TPU v7x, 32 devices: a whole 2x2x4 slice. The times are simulated.
32 devices in a mesh: date: 8 (over z, core), pix: 4 (over y, x).
Axes of the slice: x: 2, y: 2, z: 4, core: 2. Of those that a mesh axis runs over, the one named last changes fastest.
Arguments:
- bin_index: int32 [128, 262144], P('date', 'pix'), may hold values from 0 to 511
- clear_mask: bfloat16 [128, 262144], P('date', 'pix'), may hold values from 0 to 1, as said below
Outputs:
- anomaly: float32 [3, 2048], P(None, 'pix')
- tile_levels: float32 [3], replicated
Inputs may be any that keep to these rules, and one draw needn't show every extreme that they name: `clear_mask`: 0 for a cloudy observation, else a positive weight.
All inputs are finite; a program needn't handle non-finite values.
Results may differ from a plain program's by a relative error of at most 0.0003.
Values sent between devices are 32-bit elements; how exact they have to be, the bound alone decides.
No kernel may reach another device: no remote copies, remote signals or barrier semaphores. Data moves between devices by JAX's collectives and lax.ppermute only.
A program may use at most 64 MiB of HBM per device.

v0:
```python
import jax
import jax.numpy as jnp
from jax import lax
from jax.sharding import PartitionSpec as P

BINS = 512
BLOCK = 128


QUANTILES = (0.1, 0.5, 0.9)
LOW_EDGE = -1.0


def percentiles(counts, before, totals):
    target = jnp.stack([quantile * totals + 0.25 for quantile in QUANTILES])
    passed = jnp.clip(
        (target[:, :, None] - before[None]) / jnp.maximum(counts, 1.0)[None], 0.0, 1.0
    )
    return LOW_EDGE + 2.0 / BINS * jnp.sum(passed, axis=2)


def block_counts(bin_index, clear_mask, blocks):
    chosen = bin_index
    frames = chosen.shape[0]
    chosen = jnp.moveaxis(chosen.reshape(frames, blocks, BLOCK), 1, 0)
    weight = jnp.moveaxis(clear_mask.reshape(frames, blocks, BLOCK), 1, 0)
    upper_digit = chosen // 16
    lower_digit = chosen % 16
    upper_values = jnp.arange(BINS // 16, dtype=jnp.int32)
    lower_values = jnp.arange(16, dtype=jnp.int32)
    upper_table = jnp.where(
        upper_digit[:, None] == upper_values[None, :, None, None],
        weight[:, None],
        jnp.zeros((), jnp.bfloat16),
    )
    lower_table = (lower_digit[:, None] == lower_values[None, :, None, None]).astype(jnp.bfloat16)
    joint_counts = jnp.einsum(
        "ghdp,gldp->ghl", upper_table, lower_table, preferred_element_type=jnp.float32
    )
    return joint_counts.reshape(blocks, BINS)


def body(bin_index, clear_mask):
    date_devices = lax.axis_size("date")
    blocks_here = bin_index.shape[1] // BLOCK
    owned_rows = blocks_here // date_devices
    triangle = (jnp.arange(BINS)[:, None] < jnp.arange(BINS)[None, :]).astype(jnp.float32)
    owned_sums = lax.psum_scatter(
        block_counts(bin_index, clear_mask, owned_rows * lax.axis_size("date")),
        "date",
        scatter_dimension=0,
        tiled=True,
    )
    tile_counts = lax.psum(jnp.sum(owned_sums, axis=0), ("date", "pix"))
    tile_before = jnp.cumsum(tile_counts) - tile_counts
    tile_levels = percentiles(tile_counts[None], tile_before[None], jnp.sum(tile_counts)[None])[
        :, 0
    ]
    before = jnp.dot(owned_sums, triangle, precision=lax.Precision.HIGHEST)
    owned_levels = (
        percentiles(owned_sums, before, jnp.sum(owned_sums, axis=1)) - tile_levels[:, None]
    )
    anomaly = lax.all_gather(owned_levels, "date", axis=1, tiled=True)
    return (anomaly, tile_levels)


def solution(mesh):
    placed = (P("date", "pix"), P("date", "pix"))
    return jax.shard_map(
        body, mesh=mesh, in_specs=placed, out_specs=(P(None, "pix"), P()), check_vma=False
    )
```

profile of v0, /device:TPU:0, one launch (start us, length us, event | category | flops | bytes accessed | tf_op | source)
XLA Modules:
  0.0 145.4 jit_solution(10991119551946988317)
XLA Ops:
  7.2 0.0 reduce-scatter.4.cloned.1.call-start
  7.2 3.0 %copy.40 = s32[2,8,512,128]{3,2,1,0:T(8,128)S(1)} copy(s32[2,8,512,128]{3,1,2,0:T(8,128)} %bitcast.84) | data formatting | bytes 8388608
  10.2 3.8 %add_select_fusion.1 = (s32[512,16,128]{2,0,1:T(8,128)S(1)}, s32[512,16,128]{2,0,1:T(8,128)S(1)}) fusion(s32[2,8,512,128]{3,2,1,0:T(8,128)S(1)} %copy.40), kind=kLoop, calls=%fused_computation.9 | loop fusion | flops 19922944 | bytes 12582912 | tf_op jit(solution)/shard_map/jit(floor_divide)/jit(_where)/select_n | solution.py:27
  14.1 2.4 %copy.29 = s32[512,16,128]{2,1,0:T(8,128)S(1)} copy(s32[512,16,128]{2,0,1:T(8,128)S(1)} %get-tuple-element.4) | data formatting | bytes 8388608 | tf_op jit(solution)/shard_map/jit(floor_divide)/jit(_where)/select_n | solution.py:27
  16.5 0.0 copy-start
  16.5 2.4 %copy.31 = s32[512,16,128]{2,1,0:T(8,128)S(1)} copy(s32[512,16,128]{2,0,1:T(8,128)S(1)} %get-tuple-element.5) | data formatting | bytes 8388608 | tf_op jit(solution)/shard_map/jit(remainder)/select_n | solution.py:28
  18.9 0.0 copy-done
  19.0 0.4 copy.41
  19.3 1.4 copy.30
  20.7 20.1 %fusion.10 = f32[512,32,16]{1,2,0:T(8,128)} fusion(s32[512,16,128]{2,1,0:T(8,128)S(1)} %copy.31, s32[512,16,128]{2,1,0:T(8,128)S(1)} %copy.29, bf16[512,16,128]{2,1,0:T(8,128)(2,1)S(1)} %copy.30), kind=kOutput, calls=%fused_computation.18 | convolution fusion | flops 1157627904 | bytes 11534336 | tf_op jit(solution)/shard_map/ghdp,gldp->ghl/dot_general | solution.py:37
  40.8 3.2 %copy.32 = f32[512,32,16]{0,2,1:T(8,128)S(1)} copy(f32[512,32,16]{1,2,0:T(8,128)} %fusion.10) | data formatting | bytes 2097152 | tf_op jit(solution)/shard_map/ghdp,gldp->ghl/dot_general | solution.py:37
  44.0 1.3 copy.36
  45.4 0.0 reduce-scatter.4.cloned.1.call-update
  45.4 35.8 %reduce-scatter.4.cloned.1.call-done = f32[64,512]{1,0:T(8,128)} async-done(((f32[512,512]{1,0:T(8,128)}), f32[64,512]{1,0:T(8,128)}) %reduce-scatter.4.cloned.1.call-update) | async-done | bytes 131088
  81.2 1.0 fusion.15
  82.2 37.4 %psum.7 = f32[512]{0:T(512)S(1)} all-reduce(f32[512]{0:T(512)S(1)} %get-tuple-element.2), channel_id=1, replica_groups=mesh['date'=8,'pix'=4] {'date','pix'}, use_global_device_ids=true, to_apply=%region_4.5 | all-reduce | flops 512 | bytes 4096 | tf_op jit(solution)/shard_map/psum | solution.py:54
  119.6 0.3 reduce-window.9
  119.9 0.1 slice.7
  120.1 0.1 slice_reduce_fusion
  120.2 0.6 fusion.16
  122.7 0.1 maximum_bitcast_fusion
  122.8 0.2 clamp_reduce_fusion.1
  123.0 0.0 copy-start.1
  123.0 1.3 fusion.13
  124.3 0.2 clamp_reduce_fusion
  124.5 0.1 subtract_bitcast_fusion
  124.6 13.3 %all-gather = f32[8,64,3]{1,2,0:T(4,128)S(1)} all-gather(f32[1,64,3]{1,2,0:T(4,128)S(1)} %subtract_bitcast_fusion), channel_id=1, replica_groups=mesh['date'=8,'pix'=4] {'date'}, dimensions={0}, use_global_device_ids=true | all-gather | bytes 6912 | tf_op jit(solution)/shard_map/all_gather | solution.py:63
  137.9 0.7 reshape.186
  138.6 0.0 copy-done.1
  (5 shorter events, 0.1 us)
Async XLA Ops:
  7.2 74.0 %reduce-scatter.4.cloned.1.call-start = ((), (), s32[]{:S(2)}) async-start(), calls=%async_computation.1 | async-start | bytes 1179648
  16.5 2.5 %copy-start = (bf16[16,65536]{1,0:T(8,128)(2,1)S(1)}, bf16[16,65536]{1,0:T(8,128)(2,1)}, u32[]{:S(2)}) copy-start(bf16[16,65536]{1,0:T(8,128)(2,1)} %param.3) | copy-start | bytes 6291460
  123.0 15.6 %copy-start.1 = (f32[3]{0:T(128)}, f32[3]{0:T(128)S(1)}, u32[]{:S(2)}) copy-start(f32[3]{0:T(128)S(1)} %multiply_add_fusion) | copy-start | bytes 40
Sparse Core Ops, SparseCore 0:
  45.5 35.6 reduce-scatter.3
where the time goes:
time: 146 us; the launch traced here: 145 us
  blocking collectives  50.8 us (35%)
  waiting for transfers between devices  35.8 us (25%)
  matrix products  21.4 us (15%)
  between operations  16.1 us (11%)
  local copies, waits for them, and re-layouts  15 us (10%)
  other arithmetic  6.37 us (4%)
    psum x1, blocking collectives, body(): tile_counts = lax.psum(jnp.sum(owned_sums, axis=0), ('date', 'pix'))  37.4 us
    unnamed x2, waiting for transfers between devices  35.8 us
    dot_general x1, matrix products, block_counts(): jnp.einsum('ghdp,gldp->ghl', upper_table, lower_table, preferred_element_...  20.1 us
    all_gather x1, blocking collectives, body(): anomaly = lax.all_gather(owned_levels, 'date', axis=1, tiled=True)  13.3 us
    unnamed x8, local copies, waits for them, and re-layouts  5.39 us
    select_n x1, other arithmetic, block_counts(): upper_digit = chosen // 16  3.84 us
    dot_general x1, local copies, waits for them, and re-layouts, block_counts(): jnp.einsum('ghdp,gldp->ghl', upper_table, lower_table, preferred_element_...  3.23 us
  transfers between devices with their start and end apart: 1, of which 1 were waited for; matrix products, arithmetic and copies ran while one was open for 0% of the time, Pallas kernels for 0%

commit v1 on v0

v1 whole, which is shorter than its diff:
```python
import functools

import jax
import jax.numpy as jnp
from jax import lax
from jax.experimental import pallas as pl
from jax.experimental.pallas import tpu as pltpu
from jax.sharding import PartitionSpec as P

BINS = 512
BLOCK = 128
QUANTILES = (0.1, 0.5, 0.9)
LOW_EDGE = -1.0

LANES = 128
LO = 16
HI = BINS // LO
PACK = LANES // HI
TILE_ROWS = LO
INTERLEAVED = 8
FRAME_PAIR = 2


def hist_kernel(where_ref, idx_ref, weight_ref, out_ref, tile_ref, hi_ref, lo_ref, weight32_ref):
    frames, width = idx_ref.shape
    blocks = width // BLOCK
    idx = idx_ref[...]
    hi_ref[...] = (idx // LO).astype(jnp.bfloat16)
    lo_ref[...] = idx % LO
    weight32_ref[...] = weight_ref[...].astype(jnp.float32)
    lo_values = lax.broadcasted_iota(jnp.int32, (LO, BLOCK), 0)
    hi_values = lax.broadcasted_iota(jnp.int32, (HI, BLOCK), 0).astype(jnp.bfloat16)
    one = jnp.ones((HI, BLOCK), jnp.float8_e4m3fn)
    zero = jnp.zeros((HI, BLOCK), jnp.float8_e4m3fn)

    def tables(block, frame):
        lanes = pl.ds(block * BLOCK, BLOCK)
        row = pl.ds(frame, 1)
        lo = jnp.broadcast_to(lo_ref[row, lanes], (LO, BLOCK))
        hi = jnp.broadcast_to(hi_ref[row, lanes], (HI, BLOCK))
        weight = jnp.broadcast_to(weight32_ref[row, lanes], (LO, BLOCK))
        return jnp.where(lo == lo_values, weight, 0.0), jnp.where(hi == hi_values, one, zero)

    tile = jnp.zeros((LO, LANES), jnp.float32)
    for first in range(0, blocks, INTERLEAVED):
        run = range(first, min(first + INTERLEAVED, blocks))
        total = {}
        for frame in range(0, frames, FRAME_PAIR):
            for block in run:
                pairs = [tables(block, f) for f in range(frame, min(frame + FRAME_PAIR, frames))]
                part = lax.dot_general(
                    jnp.concatenate([a for a, _ in pairs], axis=1),
                    jnp.concatenate([b for _, b in pairs], axis=1),
                    (((1,), (1,)), ((), ())),
                    preferred_element_type=jnp.float32,
                )
                total[block] = total[block] + part if frame else part
        for group in range(first // PACK, (run[-1] + 1) // PACK):
            joint = jnp.concatenate([total[group * PACK + j] for j in range(PACK)], axis=1)
            out_ref[0, group] = joint
            tile = tile + joint

    @pl.when(pl.program_id(0) == 0)
    def _():
        tile_ref[...] = tile

    @pl.when(pl.program_id(0) > 0)
    def _():
        tile_ref[...] += tile


def hist(where, bin_index, clear_mask, blocks):
    frames = bin_index.shape[0]
    width = blocks * BLOCK
    runs = where.shape[0]
    groups = blocks // PACK
    taken = pl.BlockSpec((frames, width), lambda i, where: (0, where[i]))
    return pl.pallas_call(
        hist_kernel,
        grid_spec=pltpu.PrefetchScalarGridSpec(
            num_scalar_prefetch=1,
            grid=(runs,),
            in_specs=[taken, taken],
            out_specs=[
                pl.BlockSpec((1, groups, LO, LANES), lambda i, where: (i, 0, 0, 0)),
                pl.BlockSpec((LO, LANES), lambda i, where: (0, 0)),
            ],
            scratch_shapes=[
                pltpu.VMEM((frames, width), jnp.bfloat16),
                pltpu.VMEM((frames, width), jnp.int32),
                pltpu.VMEM((frames, width), jnp.float32),
            ],
        ),
        out_shape=[
            jax.ShapeDtypeStruct((runs, groups, LO, LANES), jnp.float32),
            jax.ShapeDtypeStruct((LO, LANES), jnp.float32),
        ],
        cost_estimate=pl.CostEstimate(
            flops=2 * BINS * frames * width * runs * 8,
            transcendentals=0,
            bytes_accessed=6 * frames * width * runs,
        ),
        name="hist",
    )(where, bin_index, clear_mask)


def split3(x):
    first = x.astype(jnp.bfloat16)
    rest = x - first.astype(jnp.float32)
    second = rest.astype(jnp.bfloat16)
    third = (rest - second.astype(jnp.float32)).astype(jnp.bfloat16)
    return first, second, third


def ones_where(mask):
    return jnp.where(mask, 1.0, 0.0).astype(jnp.bfloat16)


def right(x, ones):
    return sum(jnp.dot(p, ones, preferred_element_type=jnp.float32) for p in split3(x))


def left(ones, x):
    return sum(jnp.dot(ones, p, preferred_element_type=jnp.float32) for p in split3(x))


def iotas(rows, columns):
    shape = (rows, columns)
    return lax.broadcasted_iota(jnp.int32, shape, 0), lax.broadcasted_iota(jnp.int32, shape, 1)


def passed_sums(counts):
    groups = counts.shape[0]
    rows = groups * LO
    r, c = iotas(rows, rows)
    earlier_lo = ones_where((r // LO == c // LO) & (c % LO < r % LO))
    below = left(earlier_lo, counts.reshape(rows, LANES)).reshape(groups, LO, LANES)
    upper = jnp.sum(counts, axis=1)
    r, c = iotas(LANES, LANES)
    same = r // HI == c // HI
    above = right(upper, ones_where(same & (r < c)))
    totals = right(upper, ones_where(same))
    before = below + above[:, None, :]
    width = jnp.maximum(counts, 1.0)
    out = []
    for quantile in QUANTILES:
        target = quantile * totals + 0.25
        out.append(jnp.sum(jnp.clip((target[:, None, :] - before) / width, 0.0, 1.0), axis=1))
    return out


def levels_kernel(place_ref, tile_ref, *refs):
    *part_refs, out_ref = refs
    counts = part_refs[0][...]
    for ref in part_refs[1:]:
        counts = counts + ref[...]
    groups = counts.shape[0]
    blocks = groups * PACK
    sums = jnp.concatenate(passed_sums(counts), axis=0)
    row, offset = place_ref[0], place_ref[1]
    r, c = iotas(LANES, LANES)
    local = c - offset
    spread = right(sums, ones_where((local % PACK == r // HI) & (local >= 0) & (local < blocks)))
    g, c = iotas(groups, LANES)
    local = c - offset
    mine = (local // PACK == g) & (local >= 0) & (local < blocks)
    out_ref[:TILE_ROWS, :] = tile_ref[...]
    out_ref[TILE_ROWS:, :] = jnp.zeros((out_ref.shape[0] - TILE_ROWS, LANES), jnp.float32)
    rows = (out_ref.shape[0] - TILE_ROWS) // len(QUANTILES)
    for n in range(len(QUANTILES)):
        each = jnp.where(mine, spread[n * groups : (n + 1) * groups], 0.0)
        level = LOW_EDGE + 2.0 / BINS * jnp.sum(each, axis=0, keepdims=True)
        k, c = iotas(rows, LANES)
        local = c - offset
        held = (k == row) & (local >= 0) & (local < blocks)
        first = TILE_ROWS + n * rows
        out_ref[first : first + rows, :] = jnp.where(held, jnp.broadcast_to(level, (rows, LANES)), 0.0)


def final_kernel(merged_ref, anomaly_ref, tile_ref):
    r, c = iotas(LANES, LANES)
    tile = right(merged_ref[:TILE_ROWS, :], ones_where(r % HI == c % HI))
    rows = (merged_ref.shape[0] - TILE_ROWS) // len(QUANTILES)
    lane = lax.broadcasted_iota(jnp.int32, (1, LANES), 1)
    for n, sums in enumerate(passed_sums(tile[None])):
        total = jnp.sum(jnp.where(lane < HI, sums, 0.0), axis=1, keepdims=True)
        level = LOW_EDGE + 2.0 / BINS * total
        tile_ref[n : n + 1, :] = jnp.broadcast_to(level, (1, LANES))
        for m in range(rows):
            k = TILE_ROWS + n * rows + m
            anomaly_ref[n : n + 1, m * LANES : (m + 1) * LANES] = merged_ref[k : k + 1, :] - level


def power_of_two(n):
    return n & (n - 1) == 0


def sum_over(x, axis):
    n = lax.axis_size(axis)
    if not power_of_two(n):
        return lax.psum(x, axis)
    step = 1
    while step < n:
        x = x + lax.ppermute(x, axis, [(s, s ^ step) for s in range(n)])
        step *= 2
    return x


def body(bin_index, clear_mask):
    devices = lax.axis_size("date")
    here = lax.axis_index("date")
    blocks_here = bin_index.shape[1] // BLOCK
    owned = blocks_here // devices
    chips = devices // 2
    chip, core = here // 2, here % 2

    def partner(c, k):
        return c ^ k if power_of_two(chips) else (c + k) % chips

    tiles, received = [], []
    kept = None
    for k in reversed(range(chips)):
        base = 2 * partner(chip, k)
        where = jnp.stack([base + 1 - core, base + core]).astype(jnp.int32)
        counts, tile = hist(where, bin_index, clear_mask, owned)
        tiles.append(tile)
        other = lax.ppermute(counts[0], "date", [(s, s ^ 1) for s in range(devices)])
        if k:
            pairs = [(s, 2 * partner(s // 2, k) + s % 2) for s in range(devices)]
            received.append(lax.ppermute(counts[1] + other, "date", pairs))
        else:
            kept = [counts[1], other]
    tile = sum_over(sum(tiles), "pix")

    rows_each = blocks_here // LANES
    rows = -(-(TILE_ROWS + len(QUANTILES) * rows_each) // 8) * 8
    rows = TILE_ROWS + len(QUANTILES) * rows_each
    place = jnp.stack([here * owned // LANES, here * owned % LANES]).astype(jnp.int32)
    vmem = pl.BlockSpec(memory_space=pltpu.VMEM)
    merged = pl.pallas_call(
        levels_kernel,
        in_specs=[pl.BlockSpec(memory_space=pltpu.SMEM)] + [vmem] * (1 + len(kept) + len(received)),
        out_specs=vmem,
        out_shape=jax.ShapeDtypeStruct((rows, LANES), jnp.float32),
        name="levels",
    )(place, tile, *kept, *received)
    merged = sum_over(merged, "date")
    anomaly, tile_levels = pl.pallas_call(
        final_kernel,
        in_specs=[vmem],
        out_specs=[vmem, vmem],
        out_shape=[
            jax.ShapeDtypeStruct((len(QUANTILES), blocks_here), jnp.float32),
            jax.ShapeDtypeStruct((len(QUANTILES), LANES), jnp.float32),
        ],
        name="final",
    )(merged)
    return anomaly, tile_levels[:, 0]


def solution(mesh):
    placed = (P("date", "pix"), P("date", "pix"))
    return jax.shard_map(
        body, mesh=mesh, in_specs=placed, out_specs=(P(None, "pix"), P()), check_vma=False
    )
```

time: 146 us -> 69.4 us (0.48)
  blocking collectives: 50.8 us -> 0 us
  Pallas kernels: 0 us -> 30.6 us
  waiting for transfers between devices: 35.8 us -> 13.9 us
  matrix products: 21.4 us -> 0 us
  between operations: 16.1 us -> 0.77 us
  starting transfers between devices: 0.04 us -> 11.5 us
  local copies, waits for them, and re-layouts: 15 us -> 6.38 us
    psum x1 -> x0, blocking collectives: 37.4 us -> none  [body(): tile_counts = lax.psum(jnp.sum(owned_sums, axis=0), ('date', 'pix'))]
    unnamed x2 -> x0, waiting for transfers between devices: 35.8 us -> none
    pallas_call x0 -> x6, Pallas kernels: none -> 30.6 us  [the longest x4 26.4 us: hist(): pl.pallas_call(hist_kernel, grid_spec=pltpu.PrefetchScalarGridSpec(num_sc...]
    dot_general x2 -> x0, matrix products: 21.4 us -> none  [the longest x1 20.1 us: block_counts(): jnp.einsum('ghdp,gldp->ghl', upper_table, lower_table, preferred_element_...]
    ppermute x0 -> x12, waiting for transfers between devices: none -> 13.9 us  [the longest x5 12.1 us: sum_over(): x = x + lax.ppermute(x, axis, [(s, s ^ step) for s in range(n)])]
    all_gather x1 -> x0, blocking collectives: 13.3 us -> none  [body(): anomaly = lax.all_gather(owned_levels, 'date', axis=1, tiled=True)]
    ppermute x0 -> x12, starting transfers between devices: none -> 11.5 us  [the longest x3 5.84 us: body(): received.append(lax.ppermute(counts[1] + other, 'date', pairs))]
    select_n x2 -> x0, local copies, waits for them, and re-layouts: 4.86 us -> none  [the longest x1 2.43 us: block_counts(): lower_digit = chosen % 16]
  transfers between devices with their start and end apart: 1 -> 12, of which waited for: 1 -> 6; matrix products, arithmetic and copies ran while one was open for 0% -> 11% of each run, Pallas kernels for 0% -> 29%
where the time goes in v1:
time: 69.4 us; the launch traced here: 68.8 us
  Pallas kernels  30.6 us (44%)
  waiting for transfers between devices  13.9 us (20%)
  starting transfers between devices  11.5 us (17%)
  local copies, waits for them, and re-layouts  6.38 us (9%)
  other arithmetic  5.77 us (8%)
  between operations  0.77 us (1%)
    pallas_call x4, Pallas kernels, hist(): pl.pallas_call(hist_kernel, grid_spec=pltpu.PrefetchScalarGridSpec(num_sc...  26.4 us
    ppermute x5, waiting for transfers between devices, sum_over(): x = x + lax.ppermute(x, axis, [(s, s ^ step) for s in range(n)])  12.1 us
    ppermute x3, starting transfers between devices, body(): received.append(lax.ppermute(counts[1] + other, 'date', pairs))  5.84 us
    ppermute x5, starting transfers between devices, sum_over(): x = x + lax.ppermute(x, axis, [(s, s ^ step) for s in range(n)])  4.4 us
    squeeze x4, local copies, waits for them, and re-layouts, body(): counts[0]  4.37 us
    another operation x4, other arithmetic, body(): where = jnp.stack([base + 1 - core, base + core]).astype(jnp.int32)  2.47 us
    pallas_call x1, Pallas kernels, body(): pl.pallas_call(levels_kernel, in_specs=[pl.BlockSpec(memory_space=pltpu.S...  2.41 us
    add x5, other arithmetic, sum_over(): x = x + lax.ppermute(x, axis, [(s, s ^ step) for s in range(n)])  1.94 us
  transfers between devices with their start and end apart: 12, of which 6 were waited for; matrix products, arithmetic and copies ran while one was open for 11% of the time, Pallas kernels for 29%

profile of v1, /device:TPU:0, one launch (start us, length us, event | category | flops | bytes accessed | tf_op | source)
XLA Modules:
  0.0 68.8 jit_solution(1855630303562989363)
XLA Ops:
  0.7 0.6 pad_add_fusion.1.where_ref
  1.3 6.6 %hist.4 = (f32[2,16,16,128]{3,2,1,0:T(8,128)}, f32[16,128]{1,0:T(8,128)}) custom-call(s32[2]{0:T(128)} %pad_add_fusion.1.where_ref, s32[16,65536]{1,0:T(8,128)} %idx_ref.7, bf16[16,65536]{1,0:T(8,128)(2,1)} %weight_ref.7), custom_call_target="tpu_custom_call" | custom-call | flops 2147483648 | bytes 1572864 | tf_op jit(solution)/shard_map/hist/pallas_call | solution.py:78
  7.8 0.9 %slice_bitcast_fusion.2 = f32[16,16,128]{2,1,0:T(8,128)S(1)} fusion(f32[2,16,16,128]{3,2,1,0:T(8,128)} %get-tuple-element.17), kind=kLoop, calls=%fused_computation.5 | loop fusion | bytes 262144 | tf_op jit(solution)/shard_map/squeeze | solution.py:227
  9.3 0.6 pad_add_fusion.2.where_ref
  10.0 6.6 %hist.5 = (f32[2,16,16,128]{3,2,1,0:T(8,128)}, f32[16,128]{1,0:T(8,128)}) custom-call(s32[2]{0:T(128)} %pad_add_fusion.2.where_ref, s32[16,65536]{1,0:T(8,128)} %idx_ref.7, bf16[16,65536]{1,0:T(8,128)(2,1)} %weight_ref.7), custom_call_target="tpu_custom_call" | custom-call | flops 2147483648 | bytes 1572864 | tf_op jit(solution)/shard_map/hist/pallas_call | solution.py:78
  16.5 0.9 %slice_bitcast_fusion.1 = f32[16,16,128]{2,1,0:T(8,128)S(1)} fusion(f32[2,16,16,128]{3,2,1,0:T(8,128)} %get-tuple-element.18), kind=kLoop, calls=%fused_computation.4 | loop fusion | bytes 262144 | tf_op jit(solution)/shard_map/squeeze | solution.py:227
  17.5 0.6 pad_add_fusion.3.where_ref
  18.2 6.6 %hist.6 = (f32[2,16,16,128]{3,2,1,0:T(8,128)}, f32[16,128]{1,0:T(8,128)}) custom-call(s32[2]{0:T(128)} %pad_add_fusion.3.where_ref, s32[16,65536]{1,0:T(8,128)} %idx_ref.7, bf16[16,65536]{1,0:T(8,128)(2,1)} %weight_ref.7), custom_call_target="tpu_custom_call" | custom-call | flops 2147483648 | bytes 1572864 | tf_op jit(solution)/shard_map/hist/pallas_call | solution.py:78
  24.7 0.9 %slice_bitcast_fusion = f32[16,16,128]{2,1,0:T(8,128)S(1)} fusion(f32[2,16,16,128]{3,2,1,0:T(8,128)} %get-tuple-element.19), kind=kLoop, calls=%fused_computation.3 | loop fusion | bytes 262144 | tf_op jit(solution)/shard_map/squeeze | solution.py:227
  26.2 0.6 pad_add_fusion.4.where_ref
  26.8 6.7 %hist.7 = (f32[2,16,16,128]{3,2,1,0:T(8,128)}, f32[16,128]{1,0:T(8,128)}) custom-call(s32[2]{0:T(128)} %pad_add_fusion.4.where_ref, s32[16,65536]{1,0:T(8,128)} %idx_ref.7, bf16[16,65536]{1,0:T(8,128)(2,1)} %weight_ref.7), custom_call_target="tpu_custom_call" | custom-call | flops 2147483648 | bytes 1572864 | tf_op jit(solution)/shard_map/hist/pallas_call | solution.py:78
  33.5 1.6 %slice_bitcast_fusion.3 = (f32[16,16,128]{2,1,0:T(8,128)S(1)}, f32[16,16,128]{2,1,0:T(8,128)}) fusion(f32[2,16,16,128]{3,2,1,0:T(8,128)} %get-tuple-element.16), kind=kLoop, calls=%fused_computation.6 | loop fusion | bytes 524288 | tf_op jit(solution)/shard_map/squeeze | solution.py:227
  35.2 5.1 %collective-permute-start.4 = (f32[16,16,128]{2,1,0:T(8,128)S(1)}, f32[16,16,128]{2,1,0:T(8,128)S(1)}, u32[]{:S(2)}, u32[]{:S(2)}) collective-permute-start(f32[16,16,128]{2,1,0:T(8,128)S(1)} %bitcast_add_fusion.2), channel_id=1, source_target_pairs={{0,24},{4,28},{8,16},{12,20},{16,8},{20,12},{24,0},{28,4},{1,25},{... | collective-permute-start | bytes 393224 | tf_op jit(solution)/shard_map/ppermute | solution.py:230
  40.5 0.6 collective-permute-start.8
  41.1 0.7 %add_add_fusion = f32[16,128]{1,0:T(8,128)S(1)} fusion(f32[16,128]{1,0:T(8,128)} %get-tuple-element.15, f32[16,128]{1,0:T(8,128)S(1)} %copy-done.9, f32[16,128]{1,0:T(8,128)S(1)} %copy-done.7, f32[16,128]{1,0:T(8,128)S(1)} %copy-done.8), kind=kLoop, calls=%fused_computation.8 | loop fusion | flops 6144 | bytes 40960 | tf_op jit(solution)/shard_map/add | solution.py:233
  41.8 1.7 %collective-permute-start = (f32[16,128]{1,0:T(8,128)S(1)}, f32[16,128]{1,0:T(8,128)S(1)}, u32[]{:S(2)}, u32[]{:S(2)}) collective-permute-start(f32[16,128]{1,0:T(8,128)S(1)} %add_add_fusion), channel_id=1, source_target_pairs={{0,1},{1,0},{2,3},{3,2},{4,5},{5,4},{6,7},{7,6},{8,9},{9,8},{10,11... | collective-permute-start | bytes 24584 | tf_op jit(solution)/shard_map/ppermute | solution.py:204
  43.5 2.0 %collective-permute-done = f32[16,128]{1,0:T(8,128)S(1)} collective-permute-done((f32[16,128]{1,0:T(8,128)S(1)}, f32[16,128]{1,0:T(8,128)S(1)}, u32[]{:S(2)}, u32[]{:S(2)}) %collective-permute-start) | collective-permute-done | bytes 8224 | tf_op jit(solution)/shard_map/ppermute | solution.py:204
  45.5 1.7 %collective-permute-start.1 = (f32[16,128]{1,0:T(8,128)S(1)}, f32[16,128]{1,0:T(8,128)S(1)}, u32[]{:S(2)}, u32[]{:S(2)}) collective-permute-start(f32[16,128]{1,0:T(8,128)S(1)} %add.79), channel_id=1, source_target_pairs={{0,2},{1,3},{2,0},{3,1},{4,6},{5,7},{6,4},{7,5},{8,10},{9,11},{10,... | collective-permute-start | bytes 24584 | tf_op jit(solution)/shard_map/ppermute | solution.py:204
  47.2 0.6 pad_add_fusion.place_ref
  47.8 1.3 %collective-permute-done.1 = f32[16,128]{1,0:T(8,128)S(1)} collective-permute-done((f32[16,128]{1,0:T(8,128)S(1)}, f32[16,128]{1,0:T(8,128)S(1)}, u32[]{:S(2)}, u32[]{:S(2)}) %collective-permute-start.1) | collective-permute-done | bytes 8224 | tf_op jit(solution)/shard_map/ppermute | solution.py:204
  49.1 0.6 add.80.tile_ref
  49.7 1.8 %collective-permute-done.6.refs_3_ = f32[16,16,128]{2,1,0:T(8,128)S(1)} collective-permute-done((f32[16,16,128]{2,1,0:T(8,128)S(1)}, f32[16,16,128]{2,1,0:T(8,128)S(1)}, u32[]{:S(2)}, u32[]{:S(2)}) %collective-permute-start.6) | collective-permute-done | bytes 131104 | tf_op jit(solution)/shard_map/ppermute | solution.py:230
  51.6 0.6 copy-done.5
  52.3 2.4 %levels.1 = f32[28,128]{1,0:T(8,128)} custom-call(s32[2]{0:T(128)} %pad_add_fusion.place_ref, f32[16,128]{1,0:T(8,128)} %add.80.tile_ref, f32[16,16,128]{2,1,0:T(8,128)} %get-tuple-element.23.refs_0_, f32[16,16,128]{2,1,0:T(8,128)} %copy-done.3, f32[16,16,128]{2,1,0:T(8,128)} %copy-done.4, f32[16,16,128]{2,1,0:T(8,128)} %copy-done.5, f32[16,16,128]{2,1,0:T(8,128)} %copy-done.6), custom_call_target="tpu_custom_call" | custom-call | tf_op jit(solution)/shard_map/levels/pallas_call | solution.py:240
  54.7 1.4 %collective-permute-done.9 = f32[28,128]{1,0:T(8,128)S(1)} collective-permute-done((f32[28,128]{1,0:T(8,128)}, f32[28,128]{1,0:T(8,128)S(1)}, u32[]{:S(2)}, u32[]{:S(2)}) %collective-permute-start.9) | collective-permute-done | bytes 14368 | tf_op jit(solution)/shard_map/ppermute | solution.py:204
  56.1 0.7 %add.84 = f32[28,128]{1,0:T(8,128)S(1)} add(f32[28,128]{1,0:T(8,128)} %levels.1, f32[28,128]{1,0:T(8,128)S(1)} %collective-permute-done.9) | non-fusion elementwise | flops 3584 | bytes 43008 | tf_op jit(solution)/shard_map/add | solution.py:204
  56.8 3.7 %collective-permute-done.10 = f32[28,128]{1,0:T(8,128)S(1)} collective-permute-done((f32[28,128]{1,0:T(8,128)S(1)}, f32[28,128]{1,0:T(8,128)S(1)}, u32[]{:S(2)}, u32[]{:S(2)}) %collective-permute-start.10) | collective-permute-done | bytes 14368 | tf_op jit(solution)/shard_map/ppermute | solution.py:204
  60.6 1.0 %collective-permute-start.11 = (f32[28,128]{1,0:T(8,128)S(1)}, f32[28,128]{1,0:T(8,128)S(1)}, u32[]{:S(2)}, u32[]{:S(2)}) collective-permute-start(f32[28,128]{1,0:T(8,128)S(1)} %add.85), channel_id=1, source_target_pairs={{0,16},{4,20},{8,24},{12,28},{16,0},{20,4},{24,8},{28,12},{1,17},{... | collective-permute-start | bytes 43016 | tf_op jit(solution)/shard_map/ppermute | solution.py:204
  61.6 3.6 %collective-permute-done.11 = f32[28,128]{1,0:T(8,128)S(1)} collective-permute-done((f32[28,128]{1,0:T(8,128)S(1)}, f32[28,128]{1,0:T(8,128)S(1)}, u32[]{:S(2)}, u32[]{:S(2)}) %collective-permute-start.11) | collective-permute-done | bytes 14368 | tf_op jit(solution)/shard_map/ppermute | solution.py:204
  65.2 0.6 add.86.merged_ref
  65.8 1.8 %final.1 = (f32[3,512]{1,0:T(4,128)}, f32[3,128]{1,0:T(4,128)}) custom-call(f32[28,128]{1,0:T(8,128)} %add.86.merged_ref), custom_call_target="tpu_custom_call" | custom-call | tf_op jit(solution)/shard_map/final/pallas_call | solution.py:248
  67.6 1.3 %slice_reduce_fusion = f32[3]{0:T(128)} fusion(f32[3,128]{1,0:T(4,128)} %get-tuple-element.21), kind=kLoop, calls=%fused_computation.9 | loop fusion | bytes 24 | tf_op jit(solution)/shard_map/slice | solution.py:258
  (37 shorter events, 1.5 us)
Async XLA Ops:
  8.8 26.4 %collective-permute-start.3 = (f32[16,16,128]{2,1,0:T(8,128)S(1)}, f32[16,16,128]{2,1,0:T(8,128)S(1)}, u32[]{:S(2)}, u32[]{:S(2)}) collective-permute-start(f32[16,16,128]{2,1,0:T(8,128)S(1)} %slice_bitcast_fusion.2), channel_id=1, source_target_pairs={{0,4},{4,0},{8,12},{12,8},{16,20},{20,16},{24,28},{28,24},{1,5},{5... | collective-permute-start | bytes 393224 | tf_op jit(solution)/shard_map/ppermute | solution.py:227
  17.5 22.9 %collective-permute-start.5 = (f32[16,16,128]{2,1,0:T(8,128)S(1)}, f32[16,16,128]{2,1,0:T(8,128)S(1)}, u32[]{:S(2)}, u32[]{:S(2)}) collective-permute-start(f32[16,16,128]{2,1,0:T(8,128)S(1)} %slice_bitcast_fusion.1), channel_id=1, source_target_pairs={{0,4},{4,0},{8,12},{12,8},{16,20},{20,16},{24,28},{28,24},{1,5},{5... | collective-permute-start | bytes 393224 | tf_op jit(solution)/shard_map/ppermute | solution.py:227
  25.6 14.8 %collective-permute-start.7 = (f32[16,16,128]{2,1,0:T(8,128)S(1)}, f32[16,16,128]{2,1,0:T(8,128)S(1)}, u32[]{:S(2)}, u32[]{:S(2)}) collective-permute-start(f32[16,16,128]{2,1,0:T(8,128)S(1)} %slice_bitcast_fusion), channel_id=1, source_target_pairs={{0,4},{4,0},{8,12},{12,8},{16,20},{20,16},{24,28},{28,24},{1,5},{5... | collective-permute-start | bytes 393224 | tf_op jit(solution)/shard_map/ppermute | solution.py:227
  26.8 8.4 %copy-start = (f32[2,16,16,128]{3,2,1,0:T(8,128)S(1)}, f32[2,16,16,128]{3,2,1,0:T(8,128)}, u32[]{:S(2)}) copy-start(f32[2,16,16,128]{3,2,1,0:T(8,128)} %get-tuple-element.17) | copy-start | bytes 786436
  26.8 13.5 %copy-start.1 = (f32[2,16,16,128]{3,2,1,0:T(8,128)S(1)}, f32[2,16,16,128]{3,2,1,0:T(8,128)}, u32[]{:S(2)}) copy-start(f32[2,16,16,128]{3,2,1,0:T(8,128)} %get-tuple-element.18) | copy-start | bytes 786436
  26.8 13.7 %copy-start.2 = (f32[2,16,16,128]{3,2,1,0:T(8,128)S(1)}, f32[2,16,16,128]{3,2,1,0:T(8,128)}, u32[]{:S(2)}) copy-start(f32[2,16,16,128]{3,2,1,0:T(8,128)} %get-tuple-element.19) | copy-start | bytes 786436
  26.8 14.3 %copy-start.7 = (f32[16,128]{1,0:T(8,128)S(1)}, f32[16,128]{1,0:T(8,128)}, u32[]{:S(2)}) copy-start(f32[16,128]{1,0:T(8,128)} %get-tuple-element.12) | copy-start | bytes 24580
  26.8 14.3 %copy-start.8 = (f32[16,128]{1,0:T(8,128)S(1)}, f32[16,128]{1,0:T(8,128)}, u32[]{:S(2)}) copy-start(f32[16,128]{1,0:T(8,128)} %get-tuple-element.13) | copy-start | bytes 24580
  26.8 14.3 %copy-start.9 = (f32[16,128]{1,0:T(8,128)S(1)}, f32[16,128]{1,0:T(8,128)}, u32[]{:S(2)}) copy-start(f32[16,128]{1,0:T(8,128)} %get-tuple-element.14) | copy-start | bytes 24580
  35.1 14.6 %collective-permute-start.2 = (f32[16,16,128]{2,1,0:T(8,128)S(1)}, f32[16,16,128]{2,1,0:T(8,128)S(1)}, u32[]{:S(2)}, u32[]{:S(2)}) collective-permute-start(f32[16,16,128]{2,1,0:T(8,128)S(1)} %get-tuple-element.22), channel_id=1, source_target_pairs={{0,4},{4,0},{8,12},{12,8},{16,20},{20,16},{24,28},{28,24},{1,5},{5... | collective-permute-start | bytes 393224 | tf_op jit(solution)/shard_map/ppermute | solution.py:227
  35.2 14.5 %collective-permute-start.4 = (f32[16,16,128]{2,1,0:T(8,128)S(1)}, f32[16,16,128]{2,1,0:T(8,128)S(1)}, u32[]{:S(2)}, u32[]{:S(2)}) collective-permute-start(f32[16,16,128]{2,1,0:T(8,128)S(1)} %bitcast_add_fusion.2), channel_id=1, source_target_pairs={{0,24},{4,28},{8,16},{12,20},{16,8},{20,12},{24,0},{28,4},{1,25},{... | collective-permute-start | bytes 393224 | tf_op jit(solution)/shard_map/ppermute | solution.py:230
  40.4 11.2 %collective-permute-start.6 = (f32[16,16,128]{2,1,0:T(8,128)S(1)}, f32[16,16,128]{2,1,0:T(8,128)S(1)}, u32[]{:S(2)}, u32[]{:S(2)}) collective-permute-start(f32[16,16,128]{2,1,0:T(8,128)S(1)} %bitcast_add_fusion.1), channel_id=1, source_target_pairs={{0,16},{4,20},{8,24},{12,28},{16,0},{20,4},{24,8},{28,12},{1,17},{... | collective-permute-start | bytes 393224 | tf_op jit(solution)/shard_map/ppermute | solution.py:230
  40.5 11.1 %collective-permute-start.8 = (f32[16,16,128]{2,1,0:T(8,128)S(1)}, f32[16,16,128]{2,1,0:T(8,128)S(1)}, u32[]{:S(2)}, u32[]{:S(2)}) collective-permute-start(f32[16,16,128]{2,1,0:T(8,128)S(1)} %bitcast_add_fusion), channel_id=1, source_target_pairs={{0,8},{4,12},{8,0},{12,4},{16,24},{20,28},{24,16},{28,20},{1,9},{5... | collective-permute-start | bytes 393224 | tf_op jit(solution)/shard_map/ppermute | solution.py:230
  41.8 3.7 %collective-permute-start = (f32[16,128]{1,0:T(8,128)S(1)}, f32[16,128]{1,0:T(8,128)S(1)}, u32[]{:S(2)}, u32[]{:S(2)}) collective-permute-start(f32[16,128]{1,0:T(8,128)S(1)} %add_add_fusion), channel_id=1, source_target_pairs={{0,1},{1,0},{2,3},{3,2},{4,5},{5,4},{6,7},{7,6},{8,9},{9,8},{10,11... | collective-permute-start | bytes 24584 | tf_op jit(solution)/shard_map/ppermute | solution.py:204
  45.5 3.7 %collective-permute-start.1 = (f32[16,128]{1,0:T(8,128)S(1)}, f32[16,128]{1,0:T(8,128)S(1)}, u32[]{:S(2)}, u32[]{:S(2)}) collective-permute-start(f32[16,128]{1,0:T(8,128)S(1)} %add.79), channel_id=1, source_target_pairs={{0,2},{1,3},{2,0},{3,1},{4,6},{5,7},{6,4},{7,5},{8,10},{9,11},{10,... | collective-permute-start | bytes 24584 | tf_op jit(solution)/shard_map/ppermute | solution.py:204
  49.7 1.9 %copy-start.3 = (f32[16,16,128]{2,1,0:T(8,128)}, f32[16,16,128]{2,1,0:T(8,128)S(1)}, u32[]{:S(2)}) copy-start(f32[16,16,128]{2,1,0:T(8,128)S(1)} %collective-permute-done.2.refs_1_) | copy-start | bytes 393220
  49.7 1.9 %copy-start.4 = (f32[16,16,128]{2,1,0:T(8,128)}, f32[16,16,128]{2,1,0:T(8,128)S(1)}, u32[]{:S(2)}) copy-start(f32[16,16,128]{2,1,0:T(8,128)S(1)} %collective-permute-done.4.refs_2_) | copy-start | bytes 393220
  51.6 0.6 copy-start.5
  51.6 0.7 %copy-start.6 = (f32[16,16,128]{2,1,0:T(8,128)}, f32[16,16,128]{2,1,0:T(8,128)S(1)}, u32[]{:S(2)}) copy-start(f32[16,16,128]{2,1,0:T(8,128)S(1)} %collective-permute-done.8.refs_4_) | copy-start | bytes 393220
  54.7 1.4 %collective-permute-start.9 = (f32[28,128]{1,0:T(8,128)}, f32[28,128]{1,0:T(8,128)S(1)}, u32[]{:S(2)}, u32[]{:S(2)}) collective-permute-start(f32[28,128]{1,0:T(8,128)} %levels.1), channel_id=1, source_target_pairs={{0,4},{4,0},{8,12},{12,8},{16,20},{20,16},{24,28},{28,24},{1,5},{5... | collective-permute-start | bytes 43016 | tf_op jit(solution)/shard_map/ppermute | solution.py:204
  56.8 3.7 %collective-permute-start.10 = (f32[28,128]{1,0:T(8,128)S(1)}, f32[28,128]{1,0:T(8,128)S(1)}, u32[]{:S(2)}, u32[]{:S(2)}) collective-permute-start(f32[28,128]{1,0:T(8,128)S(1)} %add.84), channel_id=1, source_target_pairs={{0,8},{4,12},{8,0},{12,4},{16,24},{20,28},{24,16},{28,20},{1,9},{5... | collective-permute-start | bytes 43016 | tf_op jit(solution)/shard_map/ppermute | solution.py:204
  60.6 4.6 %collective-permute-start.11 = (f32[28,128]{1,0:T(8,128)S(1)}, f32[28,128]{1,0:T(8,128)S(1)}, u32[]{:S(2)}, u32[]{:S(2)}) collective-permute-start(f32[28,128]{1,0:T(8,128)S(1)} %add.85), channel_id=1, source_target_pairs={{0,16},{4,20},{8,24},{12,28},{16,0},{20,4},{24,8},{28,12},{1,17},{... | collective-permute-start | bytes 43016 | tf_op jit(solution)/shard_map/ppermute | solution.py:204

commit v2 on v1

v2 whole, which is shorter than its diff:
```python
import functools

import jax
import jax.numpy as jnp
from jax import lax
from jax.experimental import pallas as pl
from jax.experimental.pallas import tpu as pltpu
from jax.sharding import PartitionSpec as P

BINS = 512
BLOCK = 128
QUANTILES = (0.1, 0.5, 0.9)
LOW_EDGE = -1.0

LANES = 128
LO_BITS = 4
LO = 1 << LO_BITS
HI = BINS // LO
HI_BITS = HI.bit_length() - 1
PACK = LANES // HI
TILE_ROWS = LO
INTERLEAVED = 8
FRAME_PAIR = 2
PIECE = 32


def power_of_two(n):
    return n & (n - 1) == 0


def partner(chip, k, chips):
    return chip ^ k if power_of_two(chips) else (chip + k) % chips


def hist_kernel(sources, devices, with_tile, here_ref, idx_hbm, weight_hbm, *refs):
    refs = list(refs)
    tile_in = refs.pop(0) if with_tile else None
    outs = [refs.pop(0) for _ in range(2 * len(sources))]
    tile_ref, idx_buf, weight_buf, hi_ref, lo_ref, weight32_ref, sems = refs
    frames = idx_buf.shape[1]
    width = idx_buf.shape[2]
    pieces = idx_buf.shape[0] // len(outs)
    blocks = width // BLOCK
    here = here_ref[0]
    chip, core = here >> 1, here & 1
    copies = []
    for n in range(len(outs)):
        owner = 2 * partner(chip, sources[n // 2], devices // 2) + (core if n % 2 else 1 - core)
        for p in range(pieces):
            at = n * pieces + p
            lanes = pl.ds(pl.multiple_of((owner * pieces + p) * width, width), width)
            pair = (
                pltpu.make_async_copy(idx_hbm.at[:, lanes], idx_buf.at[at], sems.at[0, at]),
                pltpu.make_async_copy(weight_hbm.at[:, lanes], weight_buf.at[at], sems.at[1, at]),
            )
            for copy in pair:
                copy.start()
            copies.append(pair)
    lo_values = lax.broadcasted_iota(jnp.int32, (LO, BLOCK), 0)
    hi_values = lax.broadcasted_iota(jnp.int32, (HI, BLOCK), 0).astype(jnp.bfloat16)
    one = jnp.ones((HI, BLOCK), jnp.float8_e4m3fn)
    zero = jnp.zeros((HI, BLOCK), jnp.float8_e4m3fn)

    def tables(at, block, frame):
        lanes = pl.ds(block * BLOCK, BLOCK)
        row = pl.ds(frame, 1)
        lo = jnp.broadcast_to(lo_ref[at, row, lanes], (LO, BLOCK))
        hi = jnp.broadcast_to(hi_ref[at, row, lanes], (HI, BLOCK))
        weight = jnp.broadcast_to(weight32_ref[at, row, lanes], (LO, BLOCK))
        return jnp.where(lo == lo_values, weight, 0.0), jnp.where(hi == hi_values, one, zero)

    tile = tile_in[...] if with_tile else jnp.zeros((LO, LANES), jnp.float32)
    for at, pair in enumerate(copies):
        for copy in pair:
            copy.wait()
        out_ref = outs[at // pieces]
        for first in range(0, blocks, INTERLEAVED):
            run = range(first, min(first + INTERLEAVED, blocks))
            lanes = pl.ds(first * BLOCK, len(run) * BLOCK)
            idx = idx_buf[at, :, lanes]
            hi_ref[at, :, lanes] = (idx >> LO_BITS).astype(jnp.bfloat16)
            lo_ref[at, :, lanes] = idx & (LO - 1)
            weight32_ref[at, :, lanes] = weight_buf[at, :, lanes].astype(jnp.float32)
            total = {}
            for frame in range(0, frames, FRAME_PAIR):
                for block in run:
                    pairs = [tables(at, block, f) for f in range(frame, min(frame + FRAME_PAIR, frames))]
                    part = lax.dot_general(
                        jnp.concatenate([a for a, _ in pairs], axis=1),
                        jnp.concatenate([b for _, b in pairs], axis=1),
                        (((1,), (1,)), ((), ())),
                        preferred_element_type=jnp.float32,
                    )
                    total[block] = total[block] + part if frame else part
            for group in range(first // PACK, (run[-1] + 1) // PACK):
                joint = jnp.concatenate([total[group * PACK + j] for j in range(PACK)], axis=1)
                out_ref[(at % pieces) * (blocks // PACK) + group] = joint
                tile = tile + joint
    tile_ref[...] = tile


def hist(here, bin_index, clear_mask, sources, devices, tile=None):
    frames, pixels = bin_index.shape
    owned = pixels // BLOCK // devices
    blocks = min(owned, PIECE)
    width = blocks * BLOCK
    slots = 2 * len(sources) * (owned // blocks)
    any_space = pl.BlockSpec(memory_space=pl.ANY)
    vmem = pl.BlockSpec(memory_space=pltpu.VMEM)
    tiles = [] if tile is None else [tile]
    counts = jax.ShapeDtypeStruct((owned // PACK, LO, LANES), jnp.float32)
    return pl.pallas_call(
        functools.partial(hist_kernel, tuple(sources), devices, tile is not None),
        in_specs=[pl.BlockSpec(memory_space=pltpu.SMEM), any_space, any_space] + [vmem] * len(tiles),
        out_specs=[vmem] * (2 * len(sources) + 1),
        out_shape=[counts] * (2 * len(sources)) + [jax.ShapeDtypeStruct((LO, LANES), jnp.float32)],
        scratch_shapes=[
            pltpu.VMEM((slots, frames, width), jnp.int32),
            pltpu.VMEM((slots, frames, width), jnp.bfloat16),
            pltpu.VMEM((slots, frames, width), jnp.bfloat16),
            pltpu.VMEM((slots, frames, width), jnp.int32),
            pltpu.VMEM((slots, frames, width), jnp.float32),
            pltpu.SemaphoreType.DMA((2, slots)),
        ],
        cost_estimate=pl.CostEstimate(
            flops=2 * BINS * frames * width * slots * 8,
            transcendentals=0,
            bytes_accessed=6 * frames * width * slots,
        ),
        name="hist",
    )(here, bin_index, clear_mask, *tiles)


def split3(x):
    first = x.astype(jnp.bfloat16)
    rest = x - first.astype(jnp.float32)
    second = rest.astype(jnp.bfloat16)
    third = (rest - second.astype(jnp.float32)).astype(jnp.bfloat16)
    return first, second, third


def ones_where(mask):
    return jnp.where(mask, 1.0, 0.0).astype(jnp.bfloat16)


def right(x, ones):
    return sum(jnp.dot(p, ones, preferred_element_type=jnp.float32) for p in split3(x))


def left(ones, x):
    return sum(jnp.dot(ones, p, preferred_element_type=jnp.float32) for p in split3(x))


def iotas(rows, columns):
    shape = (rows, columns)
    return lax.broadcasted_iota(jnp.int32, shape, 0), lax.broadcasted_iota(jnp.int32, shape, 1)


def passed_sums(counts):
    groups = counts.shape[0]
    rows = groups * LO
    r, c = iotas(rows, rows)
    earlier_lo = ones_where((r >> LO_BITS == c >> LO_BITS) & (c < r))
    below = left(earlier_lo, counts.reshape(rows, LANES)).reshape(groups, LO, LANES)
    upper = jnp.sum(counts, axis=1)
    r, c = iotas(LANES, LANES)
    same = r >> HI_BITS == c >> HI_BITS
    above = right(upper, ones_where(same & (r < c)))
    totals = right(upper, ones_where(same))
    before = below + above[:, None, :]
    width = jnp.maximum(counts, 1.0)
    out = []
    for quantile in QUANTILES:
        target = quantile * totals + 0.25
        out.append(jnp.sum(jnp.clip((target[:, None, :] - before) / width, 0.0, 1.0), axis=1))
    return out


def levels_kernel(here_ref, tile_ref, tile_other_ref, *refs):
    *part_refs, out_ref = refs
    counts = part_refs[0][...]
    for ref in part_refs[1:]:
        counts = counts + ref[...]
    groups = counts.shape[0]
    blocks = groups * PACK
    sums = jnp.concatenate(passed_sums(counts), axis=0)
    begin = here_ref[0] * blocks
    row, offset = begin // LANES, begin % LANES
    r, c = iotas(LANES, LANES)
    local = c - offset
    spread = right(sums, ones_where((local & (PACK - 1)) == r >> HI_BITS))
    g, c = iotas(groups, LANES)
    local = c - offset
    mine = (local >= g * PACK) & (local < (g + 1) * PACK)
    out_ref[:TILE_ROWS, :] = tile_ref[...] + tile_other_ref[...]
    rows = (out_ref.shape[0] - TILE_ROWS) // len(QUANTILES)
    k, c = iotas(rows, LANES)
    local = c - offset
    held = (k == row) & (local >= 0) & (local < blocks)
    for n in range(len(QUANTILES)):
        each = jnp.where(mine, spread[n * groups : (n + 1) * groups], 0.0)
        level = LOW_EDGE + 2.0 / BINS * jnp.sum(each, axis=0, keepdims=True)
        first = TILE_ROWS + n * rows
        out_ref[first : first + rows, :] = jnp.where(held, jnp.broadcast_to(level, (rows, LANES)), 0.0)


def final_kernel(merged_ref, other_ref, anomaly_ref, tile_ref):
    r, c = iotas(LANES, LANES)
    merged = merged_ref[...] + other_ref[...]
    tile = right(merged[:TILE_ROWS, :], ones_where((r & (HI - 1)) == (c & (HI - 1))))
    rows = (merged.shape[0] - TILE_ROWS) // len(QUANTILES)
    lane = lax.broadcasted_iota(jnp.int32, (1, LANES), 1)
    levels = jnp.zeros((1, LANES), jnp.float32)
    for n, sums in enumerate(passed_sums(tile[None])):
        total = jnp.sum(jnp.where(lane < HI, sums, 0.0), axis=1, keepdims=True)
        level = LOW_EDGE + 2.0 / BINS * total
        levels = jnp.where(lane == n, level, levels)
        for m in range(rows):
            k = TILE_ROWS + n * rows + m
            anomaly_ref[n : n + 1, m * LANES : (m + 1) * LANES] = merged[k : k + 1, :] - level
    tile_ref[...] = levels[0, : len(QUANTILES)]


def swapped(x, axis, step):
    return lax.ppermute(x, axis, [(s, s ^ step) for s in range(lax.axis_size(axis))])


def sum_but_last(x, axis):
    n = lax.axis_size(axis)
    if not power_of_two(n):
        return lax.psum(x, axis), jnp.zeros_like(x)
    step = 1
    while 2 * step < n:
        x = x + swapped(x, axis, step)
        step *= 2
    return x, swapped(x, axis, step) if n > 1 else jnp.zeros_like(x)


def body(bin_index, clear_mask):
    devices = lax.axis_size("date")
    blocks_here = bin_index.shape[1] // BLOCK
    chips = devices // 2
    here = lax.axis_index("date").astype(jnp.int32)[None]

    far = list(reversed(range(2, chips)))
    near = list(reversed(range(min(2, chips))))
    received, mine = [], []
    tile = None
    for sources in (far, near):
        if not sources:
            continue
        *counts, tile = hist(here, bin_index, clear_mask, sources, devices, tile)
        others = [swapped(x, "date", 1) for x in counts[0::2]]
        sums = []
        for k, own, other in zip(sources, counts[1::2], others):
            if k:
                sums.append(own + other)
            else:
                mine = [own, other]
        here, sums = lax.optimization_barrier((here, sums))
        for k, x in zip(sources, sums):
            pairs = [(s, 2 * partner(s // 2, k, chips) + s % 2) for s in range(devices)]
            received.append(lax.ppermute(x, "date", pairs))
    tiles = sum_but_last(tile, "pix")

    rows = TILE_ROWS + len(QUANTILES) * (blocks_here // LANES)
    smem = pl.BlockSpec(memory_space=pltpu.SMEM)
    vmem = pl.BlockSpec(memory_space=pltpu.VMEM)
    parts = mine + received
    merged = pl.pallas_call(
        levels_kernel,
        in_specs=[smem] + [vmem] * (2 + len(parts)),
        out_specs=vmem,
        out_shape=jax.ShapeDtypeStruct((rows, LANES), jnp.float32),
        name="levels",
    )(here, *tiles, *parts)
    return pl.pallas_call(
        final_kernel,
        in_specs=[vmem, vmem],
        out_specs=[vmem, vmem],
        out_shape=[
            jax.ShapeDtypeStruct((len(QUANTILES), blocks_here), jnp.float32),
            jax.ShapeDtypeStruct((len(QUANTILES),), jnp.float32),
        ],
        name="final",
    )(*sum_but_last(merged, "date"))


def solution(mesh):
    placed = (P("date", "pix"), P("date", "pix"))
    return jax.shard_map(
        body, mesh=mesh, in_specs=placed, out_specs=(P(None, "pix"), P()), check_vma=False
    )
```

time: 69.4 us -> 55.1 us (0.79)
  Pallas kernels: 30.6 us -> 21.7 us
  local copies, waits for them, and re-layouts: 6.38 us -> 1.28 us
  waiting for transfers between devices: 13.9 us -> 15.5 us
  other arithmetic: 5.77 us -> 4.2 us
    pallas_call x6 -> x4, Pallas kernels: 30.6 us -> 21.7 us  [the longest x2 17.5 us: hist(): pl.pallas_call(functools.partial(hist_kernel, tuple(sources), devices, ti...]
    squeeze x4 -> x0, local copies, waits for them, and re-layouts: 4.37 us -> none  [body(): counts[0]]
    another operation x5 -> x0, other arithmetic: 3.08 us -> none  [the longest x4 2.47 us: body(): where = jnp.stack([base + 1 - core, base + core]).astype(jnp.int32)]
    ppermute x12, waiting for transfers between devices: 13.9 us -> 15.5 us  [the longest x9 13.9 us: swapped(): lax.ppermute(x, axis, [(s, s ^ step) for s in range(lax.axis_size(axis))])]
    add x9 -> x6, other arithmetic: 2.69 us -> 4.2 us  [the longest x3 2.77 us: body(): sums.append(own + other)]
    slice x1 -> x0, local copies, waits for them, and re-layouts: 1.29 us -> none  [body(): return (anomaly, tile_levels[:, 0])]
  transfers between devices with their start and end apart: 12 -> 12, of which waited for: 6 -> 7; matrix products, arithmetic and copies ran while one was open for 11% -> 5% of each run, Pallas kernels for 29% -> 0%
where the time goes in v2:
time: 55.1 us; the launch traced here: 54.6 us
  Pallas kernels  21.7 us (39%)
  waiting for transfers between devices  15.5 us (28%)
  starting transfers between devices  11.2 us (20%)
  other arithmetic  4.2 us (8%)
  local copies, waits for them, and re-layouts  1.28 us (2%)
  between operations  0.72 us (1%)
    pallas_call x2, Pallas kernels, hist(): pl.pallas_call(functools.partial(hist_kernel, tuple(sources), devices, ti...  17.5 us
    ppermute x9, waiting for transfers between devices, swapped(): lax.ppermute(x, axis, [(s, s ^ step) for s in range(lax.axis_size(axis))])  13.9 us
    ppermute x9, starting transfers between devices, swapped(): lax.ppermute(x, axis, [(s, s ^ step) for s in range(lax.axis_size(axis))])  5.67 us
    ppermute x3, starting transfers between devices, body(): received.append(lax.ppermute(x, 'date', pairs))  5.56 us
    add x3, other arithmetic, body(): sums.append(own + other)  2.77 us
    pallas_call x1, Pallas kernels, body(): pl.pallas_call(levels_kernel, in_specs=[smem] + [vmem] * (2 + len(parts))...  2.43 us
    pallas_call x1, Pallas kernels, body(): pl.pallas_call(final_kernel, in_specs=[vmem, vmem], out_specs=[vmem, vmem...  1.77 us
    ppermute x3, waiting for transfers between devices, body(): received.append(lax.ppermute(x, 'date', pairs))  1.59 us
  transfers between devices with their start and end apart: 12, of which 7 were waited for; matrix products, arithmetic and copies ran while one was open for 5% of the time, Pallas kernels for 0%

profile of v2, /device:TPU:0, one launch (start us, length us, event | category | flops | bytes accessed | tf_op | source)
XLA Modules:
  0.0 54.6 jit_solution(12286841066954545799)
XLA Ops:
  0.6 8.4 %hist.2 = (f32[16,16,128]{2,1,0:T(8,128)}, f32[16,16,128]{2,1,0:T(8,128)}, f32[16,16,128]{2,1,0:T(8,128)}, f32[16,16,128]{2,1,0:T(8,128)}, f32[16,128]{1,0:T(8,128)}) custom-call(s32[1]{0:T(128)} %bitcast.here_ref, s32[16,65536]{1,0:T(8,128)} %idx_hbm.3, bf16[16,65536]{1,0:T(8,128)(2,1)} %weight_hbm.3), custom_call_target="tpu_custom_call" | custom-call | flops 4294967296 | bytes 3145728 | tf_op jit(solution)/shard_map/hist/pallas_call | solution.py:112
  9.0 0.5 collective-permute-start.1
  9.5 0.1 collective-permute-start
  9.6 1.1 %collective-permute-done.1 = f32[16,16,128]{2,1,0:T(8,128)S(1)} collective-permute-done((f32[16,16,128]{2,1,0:T(8,128)}, f32[16,16,128]{2,1,0:T(8,128)S(1)}, u32[]{:S(2)}, u32[]{:S(2)}) %collective-permute-start.1) | collective-permute-done | bytes 131104 | tf_op jit(solution)/shard_map/ppermute | solution.py:225
  10.7 0.9 %add.19 = f32[16,16,128]{2,1,0:T(8,128)S(1)} add(f32[16,16,128]{2,1,0:T(8,128)} %get-tuple-element.19, f32[16,16,128]{2,1,0:T(8,128)S(1)} %collective-permute-done.1) | non-fusion elementwise | flops 32768 | bytes 393216 | tf_op jit(solution)/shard_map/add | solution.py:257
  11.7 0.0 collective-permute-done
  11.7 0.9 %add.18 = f32[16,16,128]{2,1,0:T(8,128)S(1)} add(f32[16,16,128]{2,1,0:T(8,128)} %get-tuple-element.17, f32[16,16,128]{2,1,0:T(8,128)S(1)} %collective-permute-done) | non-fusion elementwise | flops 32768 | bytes 393216 | tf_op jit(solution)/shard_map/add | solution.py:257
  12.6 9.1 %hist.3 = (f32[16,16,128]{2,1,0:T(8,128)}, f32[16,16,128]{2,1,0:T(8,128)}, f32[16,16,128]{2,1,0:T(8,128)}, f32[16,16,128]{2,1,0:T(8,128)}, f32[16,128]{1,0:T(8,128)}) custom-call(s32[1]{0:T(128)} %bitcast.here_ref, s32[16,65536]{1,0:T(8,128)} %idx_hbm.3, bf16[16,65536]{1,0:T(8,128)(2,1)} %weight_hbm.3, f32[16,128]{1,0:T(8,128)} %get-tuple-element.22.refs_0_), custom_call_target="tpu_custom_call" | custom-call | flops 4294967296 | bytes 3145728 | tf_op jit(solution)/shard_map/hist/pallas_call | solution.py:112
  21.7 0.3 collective-permute-start.2
  22.1 0.2 collective-permute-start.5
  22.3 4.9 %collective-permute-start.6 = (f32[16,16,128]{2,1,0:T(8,128)S(1)}, f32[16,16,128]{2,1,0:T(8,128)S(1)}, u32[]{:S(2)}, u32[]{:S(2)}) collective-permute-start(f32[16,16,128]{2,1,0:T(8,128)S(1)} %add.18), channel_id=1, source_target_pairs={{0,24},{4,28},{8,16},{12,20},{16,8},{20,12},{24,0},{28,4},{1,25},{... | collective-permute-start | bytes 393224 | tf_op jit(solution)/shard_map/ppermute | solution.py:263
  27.2 0.0 collective-permute-done.2
  27.2 0.9 %add.20 = f32[16,16,128]{2,1,0:T(8,128)S(1)} add(f32[16,16,128]{2,1,0:T(8,128)} %get-tuple-element.23, f32[16,16,128]{2,1,0:T(8,128)S(1)} %collective-permute-done.2) | non-fusion elementwise | flops 32768 | bytes 393216 | tf_op jit(solution)/shard_map/add | solution.py:257
  28.2 0.6 %collective-permute-start.8 = (f32[16,16,128]{2,1,0:T(8,128)S(1)}, f32[16,16,128]{2,1,0:T(8,128)S(1)}, u32[]{:S(2)}, u32[]{:S(2)}) collective-permute-start(f32[16,16,128]{2,1,0:T(8,128)S(1)} %add.20), channel_id=1, source_target_pairs={{0,8},{4,12},{8,0},{12,4},{16,24},{20,28},{24,16},{28,20},{1,9},{5... | collective-permute-start | bytes 393224 | tf_op jit(solution)/shard_map/ppermute | solution.py:263
  28.8 1.8 %collective-permute-start.3 = (f32[16,128]{1,0:T(8,128)}, f32[16,128]{1,0:T(8,128)S(1)}, u32[]{:S(2)}, u32[]{:S(2)}) collective-permute-start(f32[16,128]{1,0:T(8,128)} %get-tuple-element.26), channel_id=1, source_target_pairs={{0,1},{1,0},{2,3},{3,2},{4,5},{5,4},{6,7},{7,6},{8,9},{9,8},{10,11... | collective-permute-start | bytes 24584 | tf_op jit(solution)/shard_map/ppermute | solution.py:225
  30.6 2.1 %collective-permute-done.3 = f32[16,128]{1,0:T(8,128)S(1)} collective-permute-done((f32[16,128]{1,0:T(8,128)}, f32[16,128]{1,0:T(8,128)S(1)}, u32[]{:S(2)}, u32[]{:S(2)}) %collective-permute-start.3) | collective-permute-done | bytes 8224 | tf_op jit(solution)/shard_map/ppermute | solution.py:225
  32.7 0.7 %add.21.tile_ref = f32[16,128]{1,0:T(8,128)S(1)} add(f32[16,128]{1,0:T(8,128)} %get-tuple-element.26, f32[16,128]{1,0:T(8,128)S(1)} %collective-permute-done.3) | non-fusion elementwise | flops 2048 | bytes 24576 | tf_op jit(solution)/shard_map/add | solution.py:234
  33.4 1.7 %collective-permute-start.4 = (f32[16,128]{1,0:T(8,128)S(1)}, f32[16,128]{1,0:T(8,128)S(1)}, u32[]{:S(2)}, u32[]{:S(2)}) collective-permute-start(f32[16,128]{1,0:T(8,128)S(1)} %add.21.tile_ref), channel_id=1, source_target_pairs={{0,2},{1,3},{2,0},{3,1},{4,6},{5,7},{6,4},{7,5},{8,10},{9,11},{10,... | collective-permute-start | bytes 24584 | tf_op jit(solution)/shard_map/ppermute | solution.py:225
  35.1 1.9 %collective-permute-done.4.tile_other_ref = f32[16,128]{1,0:T(8,128)S(1)} collective-permute-done((f32[16,128]{1,0:T(8,128)S(1)}, f32[16,128]{1,0:T(8,128)S(1)}, u32[]{:S(2)}, u32[]{:S(2)}) %collective-permute-start.4) | collective-permute-done | bytes 8224 | tf_op jit(solution)/shard_map/ppermute | solution.py:225
  37.0 0.0 collective-permute-done.6.refs_2_
  37.0 1.6 %collective-permute-done.7.refs_3_ = f32[16,16,128]{2,1,0:T(8,128)S(1)} collective-permute-done((f32[16,16,128]{2,1,0:T(8,128)S(1)}, f32[16,16,128]{2,1,0:T(8,128)S(1)}, u32[]{:S(2)}, u32[]{:S(2)}) %collective-permute-start.7) | collective-permute-done | bytes 131104 | tf_op jit(solution)/shard_map/ppermute | solution.py:263
  38.6 0.0 collective-permute-done.8.refs_4_
  38.7 0.6 %copy-done.2 = f32[16,16,128]{2,1,0:T(8,128)} copy-done((f32[16,16,128]{2,1,0:T(8,128)}, f32[16,16,128]{2,1,0:T(8,128)S(1)}, u32[]{:S(2)}) %copy-start.2) | copy-done | bytes 131096
  39.3 0.1 copy-done.3
  39.3 2.4 %levels.1 = f32[28,128]{1,0:T(8,128)} custom-call(s32[1]{0:T(128)} %bitcast.here_ref, f32[16,128]{1,0:T(8,128)} %copy-done.5, f32[16,128]{1,0:T(8,128)} %copy-done.7, f32[16,16,128]{2,1,0:T(8,128)} %get-tuple-element.27.refs_0_, f32[16,16,128]{2,1,0:T(8,128)} %copy-done, f32[16,16,128]{2,1,0:T(8,128)} %copy-done.1, f32[16,16,128]{2,1,0:T(8,128)} %copy-done.2, ...), custom_call_target="tpu_custom_call" | custom-call | tf_op jit(solution)/shard_map/levels/pallas_call | solution.py:270
  41.8 1.4 %collective-permute-done.9 = f32[28,128]{1,0:T(8,128)S(1)} collective-permute-done((f32[28,128]{1,0:T(8,128)}, f32[28,128]{1,0:T(8,128)S(1)}, u32[]{:S(2)}, u32[]{:S(2)}) %collective-permute-start.9) | collective-permute-done | bytes 14368 | tf_op jit(solution)/shard_map/ppermute | solution.py:225
  43.2 0.7 %add.22 = f32[28,128]{1,0:T(8,128)S(1)} add(f32[28,128]{1,0:T(8,128)} %levels.1, f32[28,128]{1,0:T(8,128)S(1)} %collective-permute-done.9) | non-fusion elementwise | flops 3584 | bytes 43008 | tf_op jit(solution)/shard_map/add | solution.py:234
  43.9 3.7 %collective-permute-done.10 = f32[28,128]{1,0:T(8,128)S(1)} collective-permute-done((f32[28,128]{1,0:T(8,128)S(1)}, f32[28,128]{1,0:T(8,128)S(1)}, u32[]{:S(2)}, u32[]{:S(2)}) %collective-permute-start.10) | collective-permute-done | bytes 14368 | tf_op jit(solution)/shard_map/ppermute | solution.py:225
  47.6 1.0 %collective-permute-start.11 = (f32[28,128]{1,0:T(8,128)S(1)}, f32[28,128]{1,0:T(8,128)S(1)}, u32[]{:S(2)}, u32[]{:S(2)}) collective-permute-start(f32[28,128]{1,0:T(8,128)S(1)} %add.23.merged_ref), channel_id=1, source_target_pairs={{0,16},{4,20},{8,24},{12,28},{16,0},{20,4},{24,8},{28,12},{1,17},{... | collective-permute-start | bytes 43016 | tf_op jit(solution)/shard_map/ppermute | solution.py:225
  48.6 3.7 %collective-permute-done.11.other_ref = f32[28,128]{1,0:T(8,128)S(1)} collective-permute-done((f32[28,128]{1,0:T(8,128)S(1)}, f32[28,128]{1,0:T(8,128)S(1)}, u32[]{:S(2)}, u32[]{:S(2)}) %collective-permute-start.11) | collective-permute-done | bytes 14368 | tf_op jit(solution)/shard_map/ppermute | solution.py:225
  52.3 0.6 %copy-done.6 = f32[28,128]{1,0:T(8,128)} copy-done((f32[28,128]{1,0:T(8,128)}, f32[28,128]{1,0:T(8,128)S(1)}, u32[]{:S(2)}) %copy-start.6) | copy-done | bytes 14360
  52.9 1.8 %final.1 = (f32[3,512]{1,0:T(4,128)}, f32[3]{0:T(128)}) custom-call(f32[28,128]{1,0:T(8,128)} %copy-done.4, f32[28,128]{1,0:T(8,128)} %copy-done.6), custom_call_target="tpu_custom_call" | custom-call | tf_op jit(solution)/shard_map/final/pallas_call | solution.py:277
  (18 shorter events, 0.0 us)
Async XLA Ops:
  9.0 1.7 %collective-permute-start.1 = (f32[16,16,128]{2,1,0:T(8,128)}, f32[16,16,128]{2,1,0:T(8,128)S(1)}, u32[]{:S(2)}, u32[]{:S(2)}) collective-permute-start(f32[16,16,128]{2,1,0:T(8,128)} %get-tuple-element.20), channel_id=1, source_target_pairs={{0,4},{4,0},{8,12},{12,8},{16,20},{20,16},{24,28},{28,24},{1,5},{5... | collective-permute-start | bytes 393224 | tf_op jit(solution)/shard_map/ppermute | solution.py:225
  9.5 2.1 %collective-permute-start = (f32[16,16,128]{2,1,0:T(8,128)}, f32[16,16,128]{2,1,0:T(8,128)S(1)}, u32[]{:S(2)}, u32[]{:S(2)}) collective-permute-start(f32[16,16,128]{2,1,0:T(8,128)} %get-tuple-element.18), channel_id=1, source_target_pairs={{0,4},{4,0},{8,12},{12,8},{16,20},{20,16},{24,28},{28,24},{1,5},{5... | collective-permute-start | bytes 393224 | tf_op jit(solution)/shard_map/ppermute | solution.py:225
  21.7 5.5 %collective-permute-start.2 = (f32[16,16,128]{2,1,0:T(8,128)}, f32[16,16,128]{2,1,0:T(8,128)S(1)}, u32[]{:S(2)}, u32[]{:S(2)}) collective-permute-start(f32[16,16,128]{2,1,0:T(8,128)} %get-tuple-element.24), channel_id=1, source_target_pairs={{0,4},{4,0},{8,12},{12,8},{16,20},{20,16},{24,28},{28,24},{1,5},{5... | collective-permute-start | bytes 393224 | tf_op jit(solution)/shard_map/ppermute | solution.py:225
  22.1 14.9 %collective-permute-start.5 = (f32[16,16,128]{2,1,0:T(8,128)}, f32[16,16,128]{2,1,0:T(8,128)S(1)}, u32[]{:S(2)}, u32[]{:S(2)}) collective-permute-start(f32[16,16,128]{2,1,0:T(8,128)} %get-tuple-element.28), channel_id=1, source_target_pairs={{0,4},{4,0},{8,12},{12,8},{16,20},{20,16},{24,28},{28,24},{1,5},{5... | collective-permute-start | bytes 393224 | tf_op jit(solution)/shard_map/ppermute | solution.py:225
  22.3 14.7 %collective-permute-start.6 = (f32[16,16,128]{2,1,0:T(8,128)S(1)}, f32[16,16,128]{2,1,0:T(8,128)S(1)}, u32[]{:S(2)}, u32[]{:S(2)}) collective-permute-start(f32[16,16,128]{2,1,0:T(8,128)S(1)} %add.18), channel_id=1, source_target_pairs={{0,24},{4,28},{8,16},{12,20},{16,8},{20,12},{24,0},{28,4},{1,25},{... | collective-permute-start | bytes 393224 | tf_op jit(solution)/shard_map/ppermute | solution.py:263
  27.2 11.4 %collective-permute-start.7 = (f32[16,16,128]{2,1,0:T(8,128)S(1)}, f32[16,16,128]{2,1,0:T(8,128)S(1)}, u32[]{:S(2)}, u32[]{:S(2)}) collective-permute-start(f32[16,16,128]{2,1,0:T(8,128)S(1)} %add.19), channel_id=1, source_target_pairs={{0,16},{4,20},{8,24},{12,28},{16,0},{20,4},{24,8},{28,12},{1,17},{... | collective-permute-start | bytes 393224 | tf_op jit(solution)/shard_map/ppermute | solution.py:263
  28.2 10.5 %collective-permute-start.8 = (f32[16,16,128]{2,1,0:T(8,128)S(1)}, f32[16,16,128]{2,1,0:T(8,128)S(1)}, u32[]{:S(2)}, u32[]{:S(2)}) collective-permute-start(f32[16,16,128]{2,1,0:T(8,128)S(1)} %add.20), channel_id=1, source_target_pairs={{0,8},{4,12},{8,0},{12,4},{16,24},{20,28},{24,16},{28,20},{1,9},{5... | collective-permute-start | bytes 393224 | tf_op jit(solution)/shard_map/ppermute | solution.py:263
  28.8 3.9 %collective-permute-start.3 = (f32[16,128]{1,0:T(8,128)}, f32[16,128]{1,0:T(8,128)S(1)}, u32[]{:S(2)}, u32[]{:S(2)}) collective-permute-start(f32[16,128]{1,0:T(8,128)} %get-tuple-element.26), channel_id=1, source_target_pairs={{0,1},{1,0},{2,3},{3,2},{4,5},{5,4},{6,7},{7,6},{8,9},{9,8},{10,11... | collective-permute-start | bytes 24584 | tf_op jit(solution)/shard_map/ppermute | solution.py:225
  33.4 5.3 %copy-start.5 = (f32[16,128]{1,0:T(8,128)}, f32[16,128]{1,0:T(8,128)S(1)}, u32[]{:S(2)}) copy-start(f32[16,128]{1,0:T(8,128)S(1)} %add.21.tile_ref) | copy-start | bytes 24580
  33.4 3.7 %collective-permute-start.4 = (f32[16,128]{1,0:T(8,128)S(1)}, f32[16,128]{1,0:T(8,128)S(1)}, u32[]{:S(2)}, u32[]{:S(2)}) collective-permute-start(f32[16,128]{1,0:T(8,128)S(1)} %add.21.tile_ref), channel_id=1, source_target_pairs={{0,2},{1,3},{2,0},{3,1},{4,6},{5,7},{6,4},{7,5},{8,10},{9,11},{10,... | collective-permute-start | bytes 24584 | tf_op jit(solution)/shard_map/ppermute | solution.py:225
  37.0 1.6 %copy-start.7 = (f32[16,128]{1,0:T(8,128)}, f32[16,128]{1,0:T(8,128)S(1)}, u32[]{:S(2)}) copy-start(f32[16,128]{1,0:T(8,128)S(1)} %collective-permute-done.4.tile_other_ref) | copy-start | bytes 24580
  37.0 1.6 %copy-start = (f32[16,16,128]{2,1,0:T(8,128)}, f32[16,16,128]{2,1,0:T(8,128)S(1)}, u32[]{:S(2)}) copy-start(f32[16,16,128]{2,1,0:T(8,128)S(1)} %collective-permute-done.5.refs_1_) | copy-start | bytes 393220
  37.0 1.6 %copy-start.1 = (f32[16,16,128]{2,1,0:T(8,128)}, f32[16,16,128]{2,1,0:T(8,128)S(1)}, u32[]{:S(2)}) copy-start(f32[16,16,128]{2,1,0:T(8,128)S(1)} %collective-permute-done.6.refs_2_) | copy-start | bytes 393220
  38.6 0.6 %copy-start.2 = (f32[16,16,128]{2,1,0:T(8,128)}, f32[16,16,128]{2,1,0:T(8,128)S(1)}, u32[]{:S(2)}) copy-start(f32[16,16,128]{2,1,0:T(8,128)S(1)} %collective-permute-done.7.refs_3_) | copy-start | bytes 393220
  38.6 0.7 %copy-start.3 = (f32[16,16,128]{2,1,0:T(8,128)}, f32[16,16,128]{2,1,0:T(8,128)S(1)}, u32[]{:S(2)}) copy-start(f32[16,16,128]{2,1,0:T(8,128)S(1)} %collective-permute-done.8.refs_4_) | copy-start | bytes 393220
  41.8 1.4 %collective-permute-start.9 = (f32[28,128]{1,0:T(8,128)}, f32[28,128]{1,0:T(8,128)S(1)}, u32[]{:S(2)}, u32[]{:S(2)}) collective-permute-start(f32[28,128]{1,0:T(8,128)} %levels.1), channel_id=1, source_target_pairs={{0,4},{4,0},{8,12},{12,8},{16,20},{20,16},{24,28},{28,24},{1,5},{5... | collective-permute-start | bytes 43016 | tf_op jit(solution)/shard_map/ppermute | solution.py:225
  43.9 3.7 %collective-permute-start.10 = (f32[28,128]{1,0:T(8,128)S(1)}, f32[28,128]{1,0:T(8,128)S(1)}, u32[]{:S(2)}, u32[]{:S(2)}) collective-permute-start(f32[28,128]{1,0:T(8,128)S(1)} %add.22), channel_id=1, source_target_pairs={{0,8},{4,12},{8,0},{12,4},{16,24},{20,28},{24,16},{28,20},{1,9},{5... | collective-permute-start | bytes 43016 | tf_op jit(solution)/shard_map/ppermute | solution.py:225
  47.6 4.6 %copy-start.4 = (f32[28,128]{1,0:T(8,128)}, f32[28,128]{1,0:T(8,128)S(1)}, u32[]{:S(2)}) copy-start(f32[28,128]{1,0:T(8,128)S(1)} %add.23.merged_ref) | copy-start | bytes 43012
  47.6 4.6 %collective-permute-start.11 = (f32[28,128]{1,0:T(8,128)S(1)}, f32[28,128]{1,0:T(8,128)S(1)}, u32[]{:S(2)}, u32[]{:S(2)}) collective-permute-start(f32[28,128]{1,0:T(8,128)S(1)} %add.23.merged_ref), channel_id=1, source_target_pairs={{0,16},{4,20},{8,24},{12,28},{16,0},{20,4},{24,8},{28,12},{1,17},{... | collective-permute-start | bytes 43016 | tf_op jit(solution)/shard_map/ppermute | solution.py:225
  52.3 0.6 %copy-start.6 = (f32[28,128]{1,0:T(8,128)}, f32[28,128]{1,0:T(8,128)S(1)}, u32[]{:S(2)}) copy-start(f32[28,128]{1,0:T(8,128)S(1)} %collective-permute-done.11.other_ref) | copy-start | bytes 43012

commit v3 on v2

v3 whole, which is shorter than its diff:
```python
import functools

import jax
import jax.numpy as jnp
from jax import lax
from jax.experimental import pallas as pl
from jax.experimental.pallas import tpu as pltpu
from jax.sharding import PartitionSpec as P


BINS = 512
BLOCK = 128
QUANTILES = (0.1, 0.5, 0.9)
LOW_EDGE = -1.0

LANES = 128
LO_BITS = 4
LO = 1 << LO_BITS
HI = BINS // LO
HI_BITS = HI.bit_length() - 1
PACK = LANES // HI
TILE_ROWS = LO
INTERLEAVED = 8
FRAME_PAIR = 2
PIECE = 64


def on_chip(shape):
    return pltpu.VMEM(shape, jnp.float32)


def held(x):
    return pltpu.with_memory_space_constraint(x, pltpu.VMEM)


def power_of_two(n):
    return n & (n - 1) == 0


def partner(chip, k, chips):
    return chip ^ k if power_of_two(chips) else (chip + k) % chips


def hist_kernel(counts_here, loads, here_ref, *refs):
    refs = list(refs)
    slots, frames, width = counts_here
    blocks = width // BLOCK
    groups = blocks // PACK
    if loads:
        idx_hbm, weight_hbm = refs[:2]
        out_ref, tile_ref = refs[2:4]
        later = refs[4 : 2 + 2 * len(loads)]
        idx_buf, weight_buf, hi_ref, lo_ref, weight32_ref, sems = refs[2 + 2 * len(loads) :]
        bufs = [(idx_buf, weight_buf)] + [tuple(later[2 * n : 2 * n + 2]) for n in range(len(loads) - 1)]
        here = here_ref[0]
        chip, core = here >> 1, here & 1

        def copies(call, at, lanes):
            return (
                pltpu.make_async_copy(idx_hbm.at[:, lanes], bufs[call][0].at[at], sems.at[0, call, at]),
                pltpu.make_async_copy(weight_hbm.at[:, lanes], bufs[call][1].at[at], sems.at[1, call, at]),
            )

        def started(call):
            sources, keep, pieces, chips = loads[call]
            for n, k in enumerate(sources):
                owner = 2 * partner(chip, k, chips) + (core if keep else 1 - core)
                for p in range(pieces):
                    start = pl.multiple_of((owner * pieces + p) * width, width)
                    for copy in copies(call, n * pieces + p, pl.ds(start, width)):
                        copy.start()

        started(0)
        tile_ref[...] = jnp.zeros((LO, LANES), jnp.float32)
    else:
        idx_buf, weight_buf, tile_in, out_ref, tile_ref, hi_ref, lo_ref, weight32_ref = refs
        tile_ref[...] = tile_in[...]
    lo_values = lax.broadcasted_iota(jnp.int32, (LO, BLOCK), 0)
    hi_values = lax.broadcasted_iota(jnp.int32, (HI, BLOCK), 0).astype(jnp.bfloat16)
    one = jnp.ones((HI, BLOCK), jnp.float8_e4m3fn)
    zero = jnp.zeros((HI, BLOCK), jnp.float8_e4m3fn)

    def tables(block, frame):
        lanes = pl.ds(block * BLOCK, BLOCK)
        row = pl.ds(frame, 1)
        lo = jnp.broadcast_to(lo_ref[row, lanes], (LO, BLOCK))
        hi = jnp.broadcast_to(hi_ref[row, lanes], (HI, BLOCK))
        weight = jnp.broadcast_to(weight32_ref[row, lanes], (LO, BLOCK))
        return jnp.where(lo == lo_values, weight, 0.0), jnp.where(hi == hi_values, one, zero)

    def piece(at, unused):
        if loads:
            for copy in copies(0, at, pl.ds(0, width)):
                copy.wait()

            @pl.when(at == 0)
            def _():
                for call in range(1, len(loads)):
                    started(call)

        idx = idx_buf[at]
        hi_ref[...] = (idx >> LO_BITS).astype(jnp.bfloat16)
        lo_ref[...] = idx & (LO - 1)
        weight32_ref[...] = weight_buf[at].astype(jnp.float32)
        tile = tile_ref[...]
        for first in range(0, blocks, INTERLEAVED):
            run = range(first, min(first + INTERLEAVED, blocks))
            total = {}
            for frame in range(0, frames, FRAME_PAIR):
                for block in run:
                    pairs = [tables(block, f) for f in range(frame, min(frame + FRAME_PAIR, frames))]
                    part = lax.dot_general(
                        jnp.concatenate([a for a, _ in pairs], axis=1),
                        jnp.concatenate([b for _, b in pairs], axis=1),
                        (((1,), (1,)), ((), ())),
                        preferred_element_type=jnp.float32,
                    )
                    total[block] = total[block] + part if frame else part
            for group in range(len(run) // PACK):
                each = [total[run[group * PACK + j]] for j in range(PACK)]
                joint = jnp.concatenate(each, axis=1)
                out_ref[at * groups + first // PACK + group] = joint
                tile = tile + joint
        tile_ref[...] = tile
        return unused

    lax.fori_loop(0, slots, piece, 0)
    for call in range(1, len(loads)):
        sources, _, pieces, _ = loads[call]
        for at in range(len(sources) * pieces):
            for copy in copies(call, at, pl.ds(0, width)):
                copy.wait()


def hist(here, frames, slots, width, operands, loads=()):
    in_hbm = pl.BlockSpec(memory_space=pltpu.HBM)
    vmem = pl.BlockSpec(memory_space=pltpu.VMEM)
    groups = slots * (width // BLOCK) // PACK
    outs = [on_chip((groups, LO, LANES)), on_chip((LO, LANES))]
    scratch = [
        pltpu.VMEM((frames, width), jnp.bfloat16),
        pltpu.VMEM((frames, width), jnp.int32),
        pltpu.VMEM((frames, width), jnp.float32),
    ]
    if loads:
        for sources, _, pieces, _ in loads[1:]:
            shape = (len(sources) * pieces, frames, width)
            outs += [pltpu.VMEM(shape, jnp.int32), pltpu.VMEM(shape, jnp.bfloat16)]
        most = max(len(sources) * pieces for sources, _, pieces, _ in loads)
        scratch = [
            pltpu.VMEM((slots, frames, width), jnp.int32),
            pltpu.VMEM((slots, frames, width), jnp.bfloat16),
            *scratch,
            pltpu.SemaphoreType.DMA((2, len(loads), most)),
        ]
    return pl.pallas_call(
        functools.partial(hist_kernel, (slots, frames, width), tuple(loads)),
        in_specs=[pl.BlockSpec(memory_space=pltpu.SMEM)]
        + [in_hbm if loads else vmem] * len(operands),
        out_specs=[vmem] * len(outs),
        out_shape=outs,
        scratch_shapes=scratch,
        compiler_params=pltpu.CompilerParams(vmem_limit_bytes=24 << 20),
        cost_estimate=pl.CostEstimate(
            flops=2 * BINS * frames * width * slots * 8,
            transcendentals=0,
            bytes_accessed=6 * frames * width * slots,
        ),
        name="hist",
    )(here, *operands)


def split3(x):
    first = x.astype(jnp.bfloat16)
    rest = x - first.astype(jnp.float32)
    second = rest.astype(jnp.bfloat16)
    third = (rest - second.astype(jnp.float32)).astype(jnp.bfloat16)
    return first, second, third


def ones_where(mask):
    return jnp.where(mask, 1.0, 0.0).astype(jnp.bfloat16)


def right(x, ones):
    return sum(jnp.dot(p, ones, preferred_element_type=jnp.float32) for p in split3(x))


def left(ones, x):
    return sum(jnp.dot(ones, p, preferred_element_type=jnp.float32) for p in split3(x))


def iotas(rows, columns):
    shape = (rows, columns)
    return lax.broadcasted_iota(jnp.int32, shape, 0), lax.broadcasted_iota(jnp.int32, shape, 1)


def passed_sums(counts):
    groups = counts.shape[0]
    rows = groups * LO
    r, c = iotas(rows, rows)
    earlier_lo = ones_where((r >> LO_BITS == c >> LO_BITS) & (c < r))
    below = left(earlier_lo, counts.reshape(rows, LANES)).reshape(groups, LO, LANES)
    upper = jnp.sum(counts, axis=1)
    r, c = iotas(LANES, LANES)
    same = r >> HI_BITS == c >> HI_BITS
    above = right(upper, ones_where(same & (r < c)))
    totals = right(upper, ones_where(same))
    before = below + above[:, None, :]
    inverse = 1.0 / jnp.maximum(counts, 1.0)
    out = []
    for quantile in QUANTILES:
        target = quantile * totals + 0.25
        out.append(jnp.sum(jnp.clip((target[:, None, :] - before) * inverse, 0.0, 1.0), axis=1))
    return out


def levels_kernel(here_ref, tile_ref, tile_other_ref, *refs):
    *part_refs, out_ref = refs
    size = part_refs[-1].shape[0]
    counts = None
    for ref in part_refs:
        part = ref[ref.shape[0] - size :]
        counts = part if counts is None else counts + part
    groups = counts.shape[0]
    blocks = groups * PACK
    sums = jnp.concatenate(passed_sums(counts), axis=0)
    begin = here_ref[0] * blocks
    row, offset = begin // LANES, begin % LANES
    r, c = iotas(LANES, LANES)
    local = c - offset
    spread = right(sums, ones_where((local & (PACK - 1)) == r >> HI_BITS))
    g, c = iotas(groups, LANES)
    local = c - offset
    mine = (local >= g * PACK) & (local < (g + 1) * PACK)
    out_ref[:TILE_ROWS, :] = tile_ref[...] + tile_other_ref[...]
    rows = (out_ref.shape[0] - TILE_ROWS) // len(QUANTILES)
    k, c = iotas(rows, LANES)
    local = c - offset
    held = (k == row) & (local >= 0) & (local < blocks)
    for n in range(len(QUANTILES)):
        each = jnp.where(mine, spread[n * groups : (n + 1) * groups], 0.0)
        level = LOW_EDGE + 2.0 / BINS * jnp.sum(each, axis=0, keepdims=True)
        first = TILE_ROWS + n * rows
        out_ref[first : first + rows, :] = jnp.where(held, jnp.broadcast_to(level, (rows, LANES)), 0.0)


def final_kernel(merged_ref, other_ref, anomaly_ref, tile_ref):
    r, c = iotas(LANES, LANES)
    merged = merged_ref[...] + other_ref[...]
    tile = right(merged[:TILE_ROWS, :], ones_where((r & (HI - 1)) == (c & (HI - 1))))
    rows = (merged.shape[0] - TILE_ROWS) // len(QUANTILES)
    lane = lax.broadcasted_iota(jnp.int32, (1, LANES), 1)
    levels = jnp.zeros((1, LANES), jnp.float32)
    for n, sums in enumerate(passed_sums(tile[None])):
        total = jnp.sum(jnp.where(lane < HI, sums, 0.0), axis=1, keepdims=True)
        level = LOW_EDGE + 2.0 / BINS * total
        levels = jnp.where(lane == n, level, levels)
        for m in range(rows):
            k = TILE_ROWS + n * rows + m
            anomaly_ref[n : n + 1, m * LANES : (m + 1) * LANES] = merged[k : k + 1, :] - level
    tile_ref[...] = levels[0, : len(QUANTILES)]


def swapped(x, axis, step):
    return lax.ppermute(x, axis, [(s, s ^ step) for s in range(lax.axis_size(axis))])


def sum_but_last(x, axis):
    n = lax.axis_size(axis)
    if not power_of_two(n):
        return lax.psum(x, axis), jnp.zeros_like(x)
    step = 1
    while 2 * step < n:
        other = swapped(x, axis, step)
        x = x + other
        step *= 2
    return x, swapped(x, axis, step) if n > 1 else jnp.zeros_like(x)


def body(bin_index, clear_mask):
    devices = lax.axis_size("date")
    blocks_here = bin_index.shape[1] // BLOCK
    chips = devices // 2
    here = lax.axis_index("date").astype(jnp.int32)[None]

    frames = bin_index.shape[0]
    owned = blocks_here // devices
    owned_groups = owned // PACK
    blocks = min(owned, PIECE)
    width = blocks * BLOCK
    pieces = owned // blocks
    far = tuple(reversed(range(2, chips)))
    near = tuple(reversed(range(min(2, chips))))
    loads = [(k, keep, pieces, chips) for k in (far, near) if k for keep in (False, True)]
    stages = [k for k in (far, near) if k]

    args = [pltpu.with_memory_space_constraint(x, pltpu.HBM) for x in (bin_index, clear_mask)]
    received, mine = [], []
    tile, later = None, None
    for sources in stages:
        counts = []
        for keep in range(2):
            slots = len(sources) * pieces
            if later is None:
                part, tile, *later = hist(here, frames, slots, width, args, loads)
            else:
                operands = [held(x) for x in (*later[:2], tile)]
                later = later[2:]
                part, tile = hist(here, frames, slots, width, operands)
            counts.append(part)
            if not keep:
                other = swapped(part, "date", 1)
        own = counts[1]
        for n, k in enumerate(sources):
            rows = slice(n * owned_groups, (n + 1) * owned_groups)
            if k:
                total = own[rows] + other[rows]
                pairs = [(s, 2 * partner(s // 2, k, chips) + s % 2) for s in range(devices)]
                received.append(lax.ppermute(total, "date", pairs))
            else:
                mine = [own, other]
    tiles = sum_but_last(tile, "pix")

    rows = TILE_ROWS + len(QUANTILES) * (blocks_here // LANES)
    smem = pl.BlockSpec(memory_space=pltpu.SMEM)
    vmem = pl.BlockSpec(memory_space=pltpu.VMEM)
    parts = mine + received
    merged = pl.pallas_call(
        levels_kernel,
        in_specs=[smem] + [vmem] * (2 + len(parts)),
        out_specs=vmem,
        out_shape=on_chip((rows, LANES)),
        name="levels",
    )(here, *[held(x) for x in (*tiles, *parts)])
    return pl.pallas_call(
        final_kernel,
        in_specs=[vmem, vmem],
        out_specs=[vmem, vmem],
        out_shape=[
            jax.ShapeDtypeStruct((len(QUANTILES), blocks_here), jnp.float32),
            jax.ShapeDtypeStruct((len(QUANTILES),), jnp.float32),
        ],
        name="final",
    )(*[held(x) for x in sum_but_last(merged, "date")])


def solution(mesh):
    placed = (P("date", "pix"), P("date", "pix"))
    return jax.shard_map(body, mesh=mesh, in_specs=placed, out_specs=(P(None, "pix"), P()), check_vma=False)
```

time: 55.1 us -> 42.6 us (0.77)
  Pallas kernels: 21.7 us -> 15.1 us
  other arithmetic: 4.2 us -> 0.07 us
  waiting for transfers between devices: 15.5 us -> 11.4 us
  starting transfers between devices: 11.2 us -> 15.2 us
  local copies, waits for them, and re-layouts: 1.28 us -> 0 us
    ppermute x9 -> x7, waiting for transfers between devices: 13.9 us -> 8.45 us  [swapped(): lax.ppermute(x, axis, [(s, s ^ step) for s in range(lax.axis_size(axis))])]
    add x6 -> x5, other arithmetic: 4.2 us -> 0.07 us  [the longest x2 0.06 us: body(): total = own[rows] + other[rows]]
    pallas_call x2 -> x4, Pallas kernels: 17.5 us -> 13.4 us  [hist(): pl.pallas_call(functools.partial(hist_kernel, (slots, frames, width), tup...]
    ppermute x9 -> x7, starting transfers between devices: 5.67 us -> 9.45 us  [swapped(): lax.ppermute(x, axis, [(s, s ^ step) for s in range(lax.axis_size(axis))])]
    pallas_call x1, Pallas kernels: 2.43 us -> 0.63 us  [body(): pl.pallas_call(levels_kernel, in_specs=[smem] + [vmem] * (2 + len(parts))...]
    ppermute x3, waiting for transfers between devices: 1.59 us -> 2.98 us  [body(): received.append(lax.ppermute(total, 'date', pairs))]
    unnamed x16 -> x0, local copies, waits for them, and re-layouts: 1.28 us -> none
    pallas_call x1, Pallas kernels: 1.77 us -> 1.04 us  [body(): pl.pallas_call(final_kernel, in_specs=[vmem, vmem], out_specs=[vmem, vmem...]
  transfers between devices with their start and end apart: 12 -> 10, of which waited for: 7 -> 6; matrix products, arithmetic and copies ran while one was open for 5% -> 0% of each run, Pallas kernels for 0% -> 7%
where the time goes in v3:
time: 42.6 us; the launch traced here: 42.5 us
  starting transfers between devices  15.2 us (36%)
  Pallas kernels  15.1 us (35%)
  waiting for transfers between devices  11.4 us (27%)
  between operations  0.7 us (2%)
    pallas_call x4, Pallas kernels, hist(): pl.pallas_call(functools.partial(hist_kernel, (slots, frames, width), tup...  13.4 us
    ppermute x7, starting transfers between devices, swapped(): lax.ppermute(x, axis, [(s, s ^ step) for s in range(lax.axis_size(axis))])  9.45 us
    ppermute x7, waiting for transfers between devices, swapped(): lax.ppermute(x, axis, [(s, s ^ step) for s in range(lax.axis_size(axis))])  8.45 us
    ppermute x3, starting transfers between devices, body(): received.append(lax.ppermute(total, 'date', pairs))  5.72 us
    ppermute x3, waiting for transfers between devices, body(): received.append(lax.ppermute(total, 'date', pairs))  2.98 us
    pallas_call x1, Pallas kernels, body(): pl.pallas_call(final_kernel, in_specs=[vmem, vmem], out_specs=[vmem, vmem...  1.04 us
  transfers between devices with their start and end apart: 10, of which 6 were waited for; matrix products, arithmetic and copies ran while one was open for 0% of the time, Pallas kernels for 7%

profile of v3, /device:TPU:0, one launch (start us, length us, event | category | flops | bytes accessed | tf_op | source)
XLA Modules:
  0.0 42.5 jit_solution(15404246253751769026)
XLA Ops:
  0.6 4.8 %hist.4 = (f32[32,16,128]{2,1,0:T(8,128)S(1)}, f32[16,128]{1,0:T(8,128)S(1)}, s32[2,16,8192]{2,1,0:T(8,128)S(1)}, bf16[2,16,8192]{2,1,0:T(8,128)(2,1)S(1)}, s32[...) custom-call(s32[1]{0:T(128)} %bitcast.here_ref, ...), custom_call_target="tpu_custom_call" | custom-call | flops 2147483648 | bytes 1572864 | tf_op jit(solution)/shard_map/hist/pallas_call | solution.py:156
  5.4 2.9 %hist.5 = (f32[32,16,128]{2,1,0:T(8,128)S(1)}, f32[16,128]{1,0:T(8,128)S(1)}) custom-call(s32[1]{0:T(128)} %bitcast.here_ref, s32[2,16,8192]{2,1,0:T(8,128)S(1)} %get-tuple-element.20.refs_0_, bf16[2,16,8192]{2,1,0:T(8,128)(2,1)S(1)} %get-tuple-element.21.refs_1_, f32[16,128]{1,0:T(8,128)S(1)} %get-tuple-element.22.refs_2_), custom_call_target="tpu_custom_call" | custom-call | flops 2147483648 | bytes 1572864 | tf_op jit(solution)/shard_map/hist/pallas_call | solution.py:156
  8.3 2.9 %hist.6 = (f32[32,16,128]{2,1,0:T(8,128)S(1)}, f32[16,128]{1,0:T(8,128)S(1)}) custom-call(s32[1]{0:T(128)} %bitcast.here_ref, s32[2,16,8192]{2,1,0:T(8,128)S(1)} %get-tuple-element.18.refs_0_, bf16[2,16,8192]{2,1,0:T(8,128)(2,1)S(1)} %get-tuple-element.19.refs_1_, f32[16,128]{1,0:T(8,128)S(1)} %get-tuple-element.23.refs_2_), custom_call_target="tpu_custom_call" | custom-call | flops 2147483648 | bytes 1572864 | tf_op jit(solution)/shard_map/hist/pallas_call | solution.py:156
  11.2 0.6 %collective-permute-start.2 = (f32[32,16,128]{2,1,0:T(8,128)S(1)}, f32[32,16,128]{2,1,0:T(8,128)S(1)}, u32[]{:S(2)}, u32[]{:S(2)}) collective-permute-start(f32[32,16,128]{2,1,0:T(8,128)S(1)} %get-tuple-element.27), channel_id=1, source_target_pairs={{0,4},{4,0},{8,12},{12,8},{16,20},{20,16},{24,28},{28,24},{1,5},{5... | collective-permute-start | bytes 786440 | tf_op jit(solution)/shard_map/ppermute | solution.py:266
  11.8 0.1 collective-permute-start.3
  11.8 2.9 %hist.7 = (f32[32,16,128]{2,1,0:T(8,128)S(1)}, f32[16,128]{1,0:T(8,128)S(1)}) custom-call(s32[1]{0:T(128)} %bitcast.here_ref, s32[2,16,8192]{2,1,0:T(8,128)S(1)} %get-tuple-element.16.refs_0_, bf16[2,16,8192]{2,1,0:T(8,128)(2,1)S(1)} %get-tuple-element.17.refs_1_, f32[16,128]{1,0:T(8,128)S(1)} %get-tuple-element.24.refs_2_), custom_call_target="tpu_custom_call" | custom-call | flops 2147483648 | bytes 1572864 | tf_op jit(solution)/shard_map/hist/pallas_call | solution.py:156
  14.7 0.0 collective-permute-done.2.refs_1_
  14.8 3.1 %collective-permute-start.6 = (f32[16,16,128]{2,1,0:T(8,128)S(1)}, f32[16,16,128]{2,1,0:T(8,128)S(1)}, u32[]{:S(2)}, u32[]{:S(2)}) collective-permute-start(f32[16,16,128]{2,1,0:T(8,128)S(1)} %slice_add_fusion), channel_id=1, source_target_pairs={{0,8},{4,12},{8,0},{12,4},{16,24},{20,28},{24,16},{28,20},{1,9},{5... | collective-permute-start | bytes 393224 | tf_op jit(solution)/shard_map/ppermute | solution.py:320
  17.8 0.0 collective-permute-done.3
  17.9 2.7 %collective-permute-start.5 = (f32[16,16,128]{2,1,0:T(8,128)S(1)}, f32[16,16,128]{2,1,0:T(8,128)S(1)}, u32[]{:S(2)}, u32[]{:S(2)}) collective-permute-start(f32[16,16,128]{2,1,0:T(8,128)S(1)} %get-tuple-element.30), channel_id=1, source_target_pairs={{0,16},{4,20},{8,24},{12,28},{16,0},{20,4},{24,8},{28,12},{1,17},{... | collective-permute-start | bytes 393224 | tf_op jit(solution)/shard_map/ppermute | solution.py:320
  20.5 0.0 collective-permute-start.4
  20.5 1.7 %collective-permute-start = (f32[16,128]{1,0:T(8,128)S(1)}, f32[16,128]{1,0:T(8,128)S(1)}, u32[]{:S(2)}, u32[]{:S(2)}) collective-permute-start(f32[16,128]{1,0:T(8,128)S(1)} %get-tuple-element.25), channel_id=1, source_target_pairs={{0,1},{1,0},{2,3},{3,2},{4,5},{5,4},{6,7},{7,6},{8,9},{9,8},{10,11... | collective-permute-start | bytes 24584 | tf_op jit(solution)/shard_map/ppermute | solution.py:266
  22.3 1.9 %collective-permute-done = f32[16,128]{1,0:T(8,128)S(1)} collective-permute-done((f32[16,128]{1,0:T(8,128)S(1)}, f32[16,128]{1,0:T(8,128)S(1)}, u32[]{:S(2)}, u32[]{:S(2)}) %collective-permute-start) | collective-permute-done | bytes 8224 | tf_op jit(solution)/shard_map/ppermute | solution.py:266
  24.2 1.7 %collective-permute-start.1 = (f32[16,128]{1,0:T(8,128)S(1)}, f32[16,128]{1,0:T(8,128)S(1)}, u32[]{:S(2)}, u32[]{:S(2)}) collective-permute-start(f32[16,128]{1,0:T(8,128)S(1)} %add.18.tile_ref), channel_id=1, source_target_pairs={{0,2},{1,3},{2,0},{3,1},{4,6},{5,7},{6,4},{7,5},{8,10},{9,11},{10,... | collective-permute-start | bytes 24584 | tf_op jit(solution)/shard_map/ppermute | solution.py:266
  25.9 1.9 %collective-permute-done.1.tile_other_ref = f32[16,128]{1,0:T(8,128)S(1)} collective-permute-done((f32[16,128]{1,0:T(8,128)S(1)}, f32[16,128]{1,0:T(8,128)S(1)}, u32[]{:S(2)}, u32[]{:S(2)}) %collective-permute-start.1) | collective-permute-done | bytes 8224 | tf_op jit(solution)/shard_map/ppermute | solution.py:266
  27.8 0.0 collective-permute-done.6.refs_4_
  27.9 3.0 %collective-permute-done.5.refs_3_ = f32[16,16,128]{2,1,0:T(8,128)S(1)} collective-permute-done((f32[16,16,128]{2,1,0:T(8,128)S(1)}, f32[16,16,128]{2,1,0:T(8,128)S(1)}, u32[]{:S(2)}, u32[]{:S(2)}) %collective-permute-start.5) | collective-permute-done | bytes 131104 | tf_op jit(solution)/shard_map/ppermute | solution.py:320
  30.8 0.0 collective-permute-done.4.refs_2_
  30.8 0.6 %levels.1 = f32[28,128]{1,0:T(8,128)S(1)} custom-call(s32[1]{0:T(128)} %bitcast.here_ref, f32[16,128]{1,0:T(8,128)S(1)} %add.18.tile_ref, f32[16,128]{1,0:T(8,128)S(1)} %collective-permute-done.1.tile_other_ref, f32[32,16,128]{2,1,0:T(8,128)S(1)} %get-tuple-element.26.refs_0_, f32[32,16,128]{2,1,0:T(8,128)S(1)} %collective-permute-done.2.refs_1_, ...), custom_call_target="tpu_custom_call" | custom-call | tf_op jit(solution)/shard_map/levels/pallas_call | solution.py:329
  31.5 0.1 collective-permute-start.7
  31.5 1.2 %collective-permute-done.7 = f32[28,128]{1,0:T(8,128)S(1)} collective-permute-done((f32[28,128]{1,0:T(8,128)S(1)}, f32[28,128]{1,0:T(8,128)S(1)}, u32[]{:S(2)}, u32[]{:S(2)}) %collective-permute-start.7) | collective-permute-done | bytes 14368 | tf_op jit(solution)/shard_map/ppermute | solution.py:266
  32.7 2.2 %collective-permute-start.8 = (f32[28,128]{1,0:T(8,128)S(1)}, f32[28,128]{1,0:T(8,128)S(1)}, u32[]{:S(2)}, u32[]{:S(2)}) collective-permute-start(f32[28,128]{1,0:T(8,128)S(1)} %add.22), channel_id=1, source_target_pairs={{0,8},{4,12},{8,0},{12,4},{16,24},{20,28},{24,16},{28,20},{1,9},{5... | collective-permute-start | bytes 43016 | tf_op jit(solution)/shard_map/ppermute | solution.py:266
  35.0 1.7 %collective-permute-done.8 = f32[28,128]{1,0:T(8,128)S(1)} collective-permute-done((f32[28,128]{1,0:T(8,128)S(1)}, f32[28,128]{1,0:T(8,128)S(1)}, u32[]{:S(2)}, u32[]{:S(2)}) %collective-permute-start.8) | collective-permute-done | bytes 14368 | tf_op jit(solution)/shard_map/ppermute | solution.py:266
  36.7 3.0 %collective-permute-start.9 = (f32[28,128]{1,0:T(8,128)S(1)}, f32[28,128]{1,0:T(8,128)S(1)}, u32[]{:S(2)}, u32[]{:S(2)}) collective-permute-start(f32[28,128]{1,0:T(8,128)S(1)} %add.23.merged_ref), channel_id=1, source_target_pairs={{0,16},{4,20},{8,24},{12,28},{16,0},{20,4},{24,8},{28,12},{1,17},{... | collective-permute-start | bytes 43016 | tf_op jit(solution)/shard_map/ppermute | solution.py:266
  39.7 1.7 %collective-permute-done.9.other_ref = f32[28,128]{1,0:T(8,128)S(1)} collective-permute-done((f32[28,128]{1,0:T(8,128)S(1)}, f32[28,128]{1,0:T(8,128)S(1)}, u32[]{:S(2)}, u32[]{:S(2)}) %collective-permute-start.9) | collective-permute-done | bytes 14368 | tf_op jit(solution)/shard_map/ppermute | solution.py:266
  41.4 1.0 %final.1 = (f32[3,512]{1,0:T(4,128)}, f32[3]{0:T(128)}) custom-call(f32[28,128]{1,0:T(8,128)S(1)} %add.23.merged_ref, f32[28,128]{1,0:T(8,128)S(1)} %collective-permute-done.9.other_ref), custom_call_target="tpu_custom_call" | custom-call | tf_op jit(solution)/shard_map/final/pallas_call | solution.py:336
  (5 shorter events, 0.1 us)
Async XLA Ops:
  11.2 3.5 %collective-permute-start.2 = (f32[32,16,128]{2,1,0:T(8,128)S(1)}, f32[32,16,128]{2,1,0:T(8,128)S(1)}, u32[]{:S(2)}, u32[]{:S(2)}) collective-permute-start(f32[32,16,128]{2,1,0:T(8,128)S(1)} %get-tuple-element.27), channel_id=1, source_target_pairs={{0,4},{4,0},{8,12},{12,8},{16,20},{20,16},{24,28},{28,24},{1,5},{5... | collective-permute-start | bytes 786440 | tf_op jit(solution)/shard_map/ppermute | solution.py:266
  11.8 6.1 %collective-permute-start.3 = (f32[32,16,128]{2,1,0:T(8,128)S(1)}, f32[32,16,128]{2,1,0:T(8,128)S(1)}, u32[]{:S(2)}, u32[]{:S(2)}) collective-permute-start(f32[32,16,128]{2,1,0:T(8,128)S(1)} %get-tuple-element.29), channel_id=1, source_target_pairs={{0,4},{4,0},{8,12},{12,8},{16,20},{20,16},{24,28},{28,24},{1,5},{5... | collective-permute-start | bytes 786440 | tf_op jit(solution)/shard_map/ppermute | solution.py:266
  14.8 13.1 %collective-permute-start.6 = (f32[16,16,128]{2,1,0:T(8,128)S(1)}, f32[16,16,128]{2,1,0:T(8,128)S(1)}, u32[]{:S(2)}, u32[]{:S(2)}) collective-permute-start(f32[16,16,128]{2,1,0:T(8,128)S(1)} %slice_add_fusion), channel_id=1, source_target_pairs={{0,8},{4,12},{8,0},{12,4},{16,24},{20,28},{24,16},{28,20},{1,9},{5... | collective-permute-start | bytes 393224 | tf_op jit(solution)/shard_map/ppermute | solution.py:320
  17.9 12.9 %collective-permute-start.5 = (f32[16,16,128]{2,1,0:T(8,128)S(1)}, f32[16,16,128]{2,1,0:T(8,128)S(1)}, u32[]{:S(2)}, u32[]{:S(2)}) collective-permute-start(f32[16,16,128]{2,1,0:T(8,128)S(1)} %get-tuple-element.30), channel_id=1, source_target_pairs={{0,16},{4,20},{8,24},{12,28},{16,0},{20,4},{24,8},{28,12},{1,17},{... | collective-permute-start | bytes 393224 | tf_op jit(solution)/shard_map/ppermute | solution.py:320
  20.5 10.3 %collective-permute-start.4 = (f32[16,16,128]{2,1,0:T(8,128)S(1)}, f32[16,16,128]{2,1,0:T(8,128)S(1)}, u32[]{:S(2)}, u32[]{:S(2)}) collective-permute-start(f32[16,16,128]{2,1,0:T(8,128)S(1)} %get-tuple-element.31), channel_id=1, source_target_pairs={{0,24},{4,28},{8,16},{12,20},{16,8},{20,12},{24,0},{28,4},{1,25},{... | collective-permute-start | bytes 393224 | tf_op jit(solution)/shard_map/ppermute | solution.py:320
  20.5 3.7 %collective-permute-start = (f32[16,128]{1,0:T(8,128)S(1)}, f32[16,128]{1,0:T(8,128)S(1)}, u32[]{:S(2)}, u32[]{:S(2)}) collective-permute-start(f32[16,128]{1,0:T(8,128)S(1)} %get-tuple-element.25), channel_id=1, source_target_pairs={{0,1},{1,0},{2,3},{3,2},{4,5},{5,4},{6,7},{7,6},{8,9},{9,8},{10,11... | collective-permute-start | bytes 24584 | tf_op jit(solution)/shard_map/ppermute | solution.py:266
  24.2 3.7 %collective-permute-start.1 = (f32[16,128]{1,0:T(8,128)S(1)}, f32[16,128]{1,0:T(8,128)S(1)}, u32[]{:S(2)}, u32[]{:S(2)}) collective-permute-start(f32[16,128]{1,0:T(8,128)S(1)} %add.18.tile_ref), channel_id=1, source_target_pairs={{0,2},{1,3},{2,0},{3,1},{4,6},{5,7},{6,4},{7,5},{8,10},{9,11},{10,... | collective-permute-start | bytes 24584 | tf_op jit(solution)/shard_map/ppermute | solution.py:266
  31.5 1.2 %collective-permute-start.7 = (f32[28,128]{1,0:T(8,128)S(1)}, f32[28,128]{1,0:T(8,128)S(1)}, u32[]{:S(2)}, u32[]{:S(2)}) collective-permute-start(f32[28,128]{1,0:T(8,128)S(1)} %levels.1), channel_id=1, source_target_pairs={{0,4},{4,0},{8,12},{12,8},{16,20},{20,16},{24,28},{28,24},{1,5},{5... | collective-permute-start | bytes 43016 | tf_op jit(solution)/shard_map/ppermute | solution.py:266
  32.7 4.0 %collective-permute-start.8 = (f32[28,128]{1,0:T(8,128)S(1)}, f32[28,128]{1,0:T(8,128)S(1)}, u32[]{:S(2)}, u32[]{:S(2)}) collective-permute-start(f32[28,128]{1,0:T(8,128)S(1)} %add.22), channel_id=1, source_target_pairs={{0,8},{4,12},{8,0},{12,4},{16,24},{20,28},{24,16},{28,20},{1,9},{5... | collective-permute-start | bytes 43016 | tf_op jit(solution)/shard_map/ppermute | solution.py:266
  36.7 4.8 %collective-permute-start.9 = (f32[28,128]{1,0:T(8,128)S(1)}, f32[28,128]{1,0:T(8,128)S(1)}, u32[]{:S(2)}, u32[]{:S(2)}) collective-permute-start(f32[28,128]{1,0:T(8,128)S(1)} %add.23.merged_ref), channel_id=1, source_target_pairs={{0,16},{4,20},{8,24},{12,28},{16,0},{20,4},{24,8},{28,12},{1,17},{... | collective-permute-start | bytes 43016 | tf_op jit(solution)/shard_map/ppermute | solution.py:266

commit v4 on v3

--- a/solution.py
+++ b/solution.py
@@ -41,17 +41,22 @@
     return chip ^ k if power_of_two(chips) else (chip + k) % chips
 
 
-def hist_kernel(counts_here, loads, here_ref, *refs):
+def hist_kernel(counts_here, own, loads, here_ref, *refs):
     refs = list(refs)
     slots, frames, width = counts_here
     blocks = width // BLOCK
     groups = blocks // PACK
-    if loads:
-        idx_hbm, weight_hbm = refs[:2]
-        out_ref, tile_ref = refs[2:4]
-        later = refs[4 : 2 + 2 * len(loads)]
-        idx_buf, weight_buf, hi_ref, lo_ref, weight32_ref, sems = refs[2 + 2 * len(loads) :]
-        bufs = [(idx_buf, weight_buf)] + [tuple(later[2 * n : 2 * n + 2]) for n in range(len(loads) - 1)]
+    idx_hbm, weight_hbm = (refs.pop(0), refs.pop(0)) if own or loads else (None, None)
+    idx_buf, weight_buf, tile_in = (None,) * 3 if own else (refs.pop(0), refs.pop(0), refs.pop(0))
+    out_ref, tile_ref = refs.pop(0), refs.pop(0)
+    bufs = [(refs.pop(0), refs.pop(0)) for _ in loads]
+    if own:
+        idx_buf, weight_buf = refs.pop(0), refs.pop(0)
+    hi_ref, lo_ref, weight32_ref = refs[:3]
+    bufs.append((idx_buf, weight_buf))
+    wanted = [*loads, own]
+    if own or loads:
+        sems = refs[3]
         here = here_ref[0]
         chip, core = here >> 1, here & 1
 
@@ -62,7 +67,7 @@
             )
 
         def started(call):
-            sources, keep, pieces, chips = loads[call]
+            sources, keep, pieces, chips = wanted[call]
             for n, k in enumerate(sources):
                 owner = 2 * partner(chip, k, chips) + (core if keep else 1 - core)
                 for p in range(pieces):
@@ -70,11 +75,12 @@
                     for copy in copies(call, n * pieces + p, pl.ds(start, width)):
                         copy.start()
 
-        started(0)
-        tile_ref[...] = jnp.zeros((LO, LANES), jnp.float32)
-    else:
-        idx_buf, weight_buf, tile_in, out_ref, tile_ref, hi_ref, lo_ref, weight32_ref = refs
-        tile_ref[...] = tile_in[...]
+        if own:
+            started(len(loads))
+        else:
+            for call in range(len(loads)):
+                started(call)
+    tile_ref[...] = jnp.zeros((LO, LANES), jnp.float32) if own else tile_in[...]
     lo_values = lax.broadcasted_iota(jnp.int32, (LO, BLOCK), 0)
     hi_values = lax.broadcasted_iota(jnp.int32, (HI, BLOCK), 0).astype(jnp.bfloat16)
     one = jnp.ones((HI, BLOCK), jnp.float8_e4m3fn)
@@ -89,13 +95,13 @@
         return jnp.where(lo == lo_values, weight, 0.0), jnp.where(hi == hi_values, one, zero)
 
     def piece(at, unused):
-        if loads:
-            for copy in copies(0, at, pl.ds(0, width)):
+        if own:
+            for copy in copies(len(loads), at, pl.ds(0, width)):
                 copy.wait()
 
             @pl.when(at == 0)
             def _():
-                for call in range(1, len(loads)):
+                for call in range(len(loads)):
                     started(call)
 
         idx = idx_buf[at]
@@ -125,14 +131,14 @@
         return unused
 
     lax.fori_loop(0, slots, piece, 0)
-    for call in range(1, len(loads)):
+    for call in range(len(loads)):
         sources, _, pieces, _ = loads[call]
         for at in range(len(sources) * pieces):
             for copy in copies(call, at, pl.ds(0, width)):
                 copy.wait()
 
 
-def hist(here, frames, slots, width, operands, loads=()):
+def hist(here, frames, slots, width, in_place, operands, own, loads):
     in_hbm = pl.BlockSpec(memory_space=pltpu.HBM)
     vmem = pl.BlockSpec(memory_space=pltpu.VMEM)
     groups = slots * (width // BLOCK) // PACK
@@ -142,21 +148,26 @@
         pltpu.VMEM((frames, width), jnp.int32),
         pltpu.VMEM((frames, width), jnp.float32),
     ]
-    if loads:
-        for sources, _, pieces, _ in loads[1:]:
-            shape = (len(sources) * pieces, frames, width)
-            outs += [pltpu.VMEM(shape, jnp.int32), pltpu.VMEM(shape, jnp.bfloat16)]
-        most = max(len(sources) * pieces for sources, _, pieces, _ in loads)
+    wanted = [*loads, own] if own else list(loads)
+    for sources, _, pieces, _ in loads:
+        shape = (len(sources) * pieces, frames, width)
+        outs += [pltpu.VMEM(shape, jnp.int32), pltpu.VMEM(shape, jnp.bfloat16)]
+    if own:
         scratch = [
             pltpu.VMEM((slots, frames, width), jnp.int32),
             pltpu.VMEM((slots, frames, width), jnp.bfloat16),
             *scratch,
-            pltpu.SemaphoreType.DMA((2, len(loads), most)),
         ]
+    if wanted:
+        most = max(len(sources) * pieces for sources, _, pieces, _ in wanted)
+        scratch.append(pltpu.SemaphoreType.DMA((2, len(wanted), most)))
+    else:
+        in_place = ()
     return pl.pallas_call(
-        functools.partial(hist_kernel, (slots, frames, width), tuple(loads)),
+        functools.partial(hist_kernel, (slots, frames, width), own, tuple(loads)),
         in_specs=[pl.BlockSpec(memory_space=pltpu.SMEM)]
-        + [in_hbm if loads else vmem] * len(operands),
+        + [in_hbm] * len(in_place)
+        + [vmem] * len(operands),
         out_specs=[vmem] * len(outs),
         out_shape=outs,
         scratch_shapes=scratch,
@@ -167,7 +178,7 @@
             bytes_accessed=6 * frames * width * slots,
         ),
         name="hist",
-    )(here, *operands)
+    )(here, *in_place, *operands)
 
 
 def split3(x):
@@ -298,16 +309,16 @@
     args = [pltpu.with_memory_space_constraint(x, pltpu.HBM) for x in (bin_index, clear_mask)]
     received, mine = [], []
     tile, later = None, None
-    for sources in stages:
+    for stage, sources in enumerate(stages):
         counts = []
         for keep in range(2):
             slots = len(sources) * pieces
-            if later is None:
-                part, tile, *later = hist(here, frames, slots, width, args, loads)
-            else:
-                operands = [held(x) for x in (*later[:2], tile)]
-                later = later[2:]
-                part, tile = hist(here, frames, slots, width, operands)
+            calls = loads[2 * stage + keep :]
+            own = calls[0] if later is None else None
+            coming = {0: calls[1:2], 1: calls[1:]}.get(2 * stage + keep, [])
+            operands = [] if own else [held(x) for x in (*later[:2], tile)]
+            part, tile, *brought = hist(here, frames, slots, width, args, operands, own, coming)
+            later = (later or [])[2:] + brought
             counts.append(part)
             if not keep:
                 other = swapped(part, "date", 1)

time: 42.6 us -> 41.6 us (0.977)
  waiting for transfers between devices: 11.4 us -> 10.7 us
  Pallas kernels: 15.1 us -> 14.5 us
    ppermute x3, waiting for transfers between devices: 2.98 us -> 1.82 us  [body(): received.append(lax.ppermute(total, 'date', pairs))]
    pallas_call x4, Pallas kernels: 13.4 us -> 12.8 us  [hist(): pl.pallas_call(functools.partial(hist_kernel, (slots, frames, width), own...]
    ppermute x7, waiting for transfers between devices: 8.45 us -> 8.91 us  [swapped(): lax.ppermute(x, axis, [(s, s ^ step) for s in range(lax.axis_size(axis))])]
  transfers between devices with their start and end apart: 10 -> 10, of which waited for: 6 -> 7; matrix products, arithmetic and copies ran while one was open for 0% -> 0% of each run, Pallas kernels for 7% -> 21%
where the time goes in v4:
time: 41.6 us; the launch traced here: 41.5 us
  starting transfers between devices  15.5 us (37%)
  Pallas kernels  14.5 us (35%)
  waiting for transfers between devices  10.7 us (26%)
  between operations  0.7 us (2%)
    pallas_call x4, Pallas kernels, hist(): pl.pallas_call(functools.partial(hist_kernel, (slots, frames, width), own...  12.8 us
    ppermute x7, starting transfers between devices, swapped(): lax.ppermute(x, axis, [(s, s ^ step) for s in range(lax.axis_size(axis))])  9.76 us
    ppermute x7, waiting for transfers between devices, swapped(): lax.ppermute(x, axis, [(s, s ^ step) for s in range(lax.axis_size(axis))])  8.91 us
    ppermute x3, starting transfers between devices, body(): received.append(lax.ppermute(total, 'date', pairs))  5.74 us
    ppermute x3, waiting for transfers between devices, body(): received.append(lax.ppermute(total, 'date', pairs))  1.82 us
    pallas_call x1, Pallas kernels, body(): pl.pallas_call(final_kernel, in_specs=[vmem, vmem], out_specs=[vmem, vmem...  1.04 us
  transfers between devices with their start and end apart: 10, of which 7 were waited for; matrix products, arithmetic and copies ran while one was open for 0% of the time, Pallas kernels for 21%

profile of v4, /device:TPU:0, one launch (start us, length us, event | category | flops | bytes accessed | tf_op | source)
XLA Modules:
  0.0 41.5 jit_solution(1140889012663247688)
XLA Ops:
  0.6 4.0 %hist.4 = (f32[32,16,128]{2,1,0:T(8,128)S(1)}, f32[16,128]{1,0:T(8,128)S(1)}, s32[2,16,8192]{2,1,0:T(8,128)S(1)}, bf16[2,16,8192]{2,1,0:T(8,128)(2,1)S(1)}) custom-call(s32[1]{0:T(128)} %bitcast.here_ref, s32[16,65536]{1,0:T(8,128)} %refs_0_.3, bf16[16,65536]{1,0:T(8,128)(2,1)} %refs_1_.3), custom_call_target="tpu_custom_call" | custom-call | flops 2147483648 | bytes 1572864 | tf_op jit(solution)/shard_map/hist/pallas_call | solution.py:166
  4.7 0.6 %collective-permute-start.3 = (f32[32,16,128]{2,1,0:T(8,128)S(1)}, f32[32,16,128]{2,1,0:T(8,128)S(1)}, u32[]{:S(2)}, u32[]{:S(2)}) collective-permute-start(f32[32,16,128]{2,1,0:T(8,128)S(1)} %get-tuple-element.29), channel_id=1, source_target_pairs={{0,4},{4,0},{8,12},{12,8},{16,20},{20,16},{24,28},{28,24},{1,5},{5... | collective-permute-start | bytes 786440 | tf_op jit(solution)/shard_map/ppermute | solution.py:277
  5.3 3.0 %hist.5 = (f32[32,16,128]{2,1,0:T(8,128)S(1)}, f32[16,128]{1,0:T(8,128)S(1)}, s32[2,16,8192]{2,1,0:T(8,128)S(1)}, bf16[2,16,8192]{2,1,0:T(8,128)(2,1)S(1)}, s32[...) custom-call(s32[1]{0:T(128)} %bitcast.here_ref, s32[16,65536]{1,0:T(8,128)} %refs_0_.3, ...), custom_call_target="tpu_custom_call" | custom-call | flops 2147483648 | bytes 1572864 | tf_op jit(solution)/shard_map/hist/pallas_call | solution.py:166
  8.2 2.9 %hist.6 = (f32[32,16,128]{2,1,0:T(8,128)S(1)}, f32[16,128]{1,0:T(8,128)S(1)}) custom-call(s32[1]{0:T(128)} %bitcast.here_ref, s32[2,16,8192]{2,1,0:T(8,128)S(1)} %get-tuple-element.21.refs_0_, bf16[2,16,8192]{2,1,0:T(8,128)(2,1)S(1)} %get-tuple-element.22.refs_1_, f32[16,128]{1,0:T(8,128)S(1)} %get-tuple-element.23.refs_2_), custom_call_target="tpu_custom_call" | custom-call | flops 2147483648 | bytes 1572864 | tf_op jit(solution)/shard_map/hist/pallas_call | solution.py:166
  11.1 0.1 collective-permute-start.2
  11.2 2.9 %hist.7 = (f32[32,16,128]{2,1,0:T(8,128)S(1)}, f32[16,128]{1,0:T(8,128)S(1)}) custom-call(s32[1]{0:T(128)} %bitcast.here_ref, s32[2,16,8192]{2,1,0:T(8,128)S(1)} %get-tuple-element.19.refs_0_, bf16[2,16,8192]{2,1,0:T(8,128)(2,1)S(1)} %get-tuple-element.20.refs_1_, f32[16,128]{1,0:T(8,128)S(1)} %get-tuple-element.24.refs_2_), custom_call_target="tpu_custom_call" | custom-call | flops 2147483648 | bytes 1572864 | tf_op jit(solution)/shard_map/hist/pallas_call | solution.py:166
  14.1 0.0 collective-permute-done.3
  14.2 4.1 %collective-permute-start.5 = (f32[16,16,128]{2,1,0:T(8,128)S(1)}, f32[16,16,128]{2,1,0:T(8,128)S(1)}, u32[]{:S(2)}, u32[]{:S(2)}) collective-permute-start(f32[16,16,128]{2,1,0:T(8,128)S(1)} %get-tuple-element.30), channel_id=1, source_target_pairs={{0,16},{4,20},{8,24},{12,28},{16,0},{20,4},{24,8},{28,12},{1,17},{... | collective-permute-start | bytes 393224 | tf_op jit(solution)/shard_map/ppermute | solution.py:331
  18.3 1.4 %collective-permute-start.4 = (f32[16,16,128]{2,1,0:T(8,128)S(1)}, f32[16,16,128]{2,1,0:T(8,128)S(1)}, u32[]{:S(2)}, u32[]{:S(2)}) collective-permute-start(f32[16,16,128]{2,1,0:T(8,128)S(1)} %get-tuple-element.31), channel_id=1, source_target_pairs={{0,24},{4,28},{8,16},{12,20},{16,8},{20,12},{24,0},{28,4},{1,25},{... | collective-permute-start | bytes 393224 | tf_op jit(solution)/shard_map/ppermute | solution.py:331
  19.6 0.0 collective-permute-done.2.refs_1_
  19.7 0.3 collective-permute-start.6
  20.0 1.5 %collective-permute-start = (f32[16,128]{1,0:T(8,128)S(1)}, f32[16,128]{1,0:T(8,128)S(1)}, u32[]{:S(2)}, u32[]{:S(2)}) collective-permute-start(f32[16,128]{1,0:T(8,128)S(1)} %get-tuple-element.25), channel_id=1, source_target_pairs={{0,1},{1,0},{2,3},{3,2},{4,5},{5,4},{6,7},{7,6},{8,9},{9,8},{10,11... | collective-permute-start | bytes 24584 | tf_op jit(solution)/shard_map/ppermute | solution.py:277
  21.4 2.2 %collective-permute-done = f32[16,128]{1,0:T(8,128)S(1)} collective-permute-done((f32[16,128]{1,0:T(8,128)S(1)}, f32[16,128]{1,0:T(8,128)S(1)}, u32[]{:S(2)}, u32[]{:S(2)}) %collective-permute-start) | collective-permute-done | bytes 8224 | tf_op jit(solution)/shard_map/ppermute | solution.py:277
  23.6 1.5 %collective-permute-start.1 = (f32[16,128]{1,0:T(8,128)S(1)}, f32[16,128]{1,0:T(8,128)S(1)}, u32[]{:S(2)}, u32[]{:S(2)}) collective-permute-start(f32[16,128]{1,0:T(8,128)S(1)} %add.18.tile_ref), channel_id=1, source_target_pairs={{0,2},{1,3},{2,0},{3,1},{4,6},{5,7},{6,4},{7,5},{8,10},{9,11},{10,... | collective-permute-start | bytes 24584 | tf_op jit(solution)/shard_map/ppermute | solution.py:277
  25.1 2.1 %collective-permute-done.1.tile_other_ref = f32[16,128]{1,0:T(8,128)S(1)} collective-permute-done((f32[16,128]{1,0:T(8,128)S(1)}, f32[16,128]{1,0:T(8,128)S(1)}, u32[]{:S(2)}, u32[]{:S(2)}) %collective-permute-start.1) | collective-permute-done | bytes 8224 | tf_op jit(solution)/shard_map/ppermute | solution.py:277
  27.3 1.0 %collective-permute-done.5.refs_3_ = f32[16,16,128]{2,1,0:T(8,128)S(1)} collective-permute-done((f32[16,16,128]{2,1,0:T(8,128)S(1)}, f32[16,16,128]{2,1,0:T(8,128)S(1)}, u32[]{:S(2)}, u32[]{:S(2)}) %collective-permute-start.5) | collective-permute-done | bytes 131104 | tf_op jit(solution)/shard_map/ppermute | solution.py:331
  28.3 0.0 collective-permute-done.4.refs_2_
  28.3 0.8 %collective-permute-done.6.refs_4_ = f32[16,16,128]{2,1,0:T(8,128)S(1)} collective-permute-done((f32[16,16,128]{2,1,0:T(8,128)S(1)}, f32[16,16,128]{2,1,0:T(8,128)S(1)}, u32[]{:S(2)}, u32[]{:S(2)}) %collective-permute-start.6) | collective-permute-done | bytes 131104 | tf_op jit(solution)/shard_map/ppermute | solution.py:331
  29.1 0.6 %levels.1 = f32[28,128]{1,0:T(8,128)S(1)} custom-call(s32[1]{0:T(128)} %bitcast.here_ref, f32[16,128]{1,0:T(8,128)S(1)} %add.18.tile_ref, f32[16,128]{1,0:T(8,128)S(1)} %collective-permute-done.1.tile_other_ref, f32[32,16,128]{2,1,0:T(8,128)S(1)} %get-tuple-element.26.refs_0_, f32[32,16,128]{2,1,0:T(8,128)S(1)} %collective-permute-done.2.refs_1_, ...), custom_call_target="tpu_custom_call" | custom-call | tf_op jit(solution)/shard_map/levels/pallas_call | solution.py:340
  29.7 0.1 collective-permute-start.7
  29.8 1.2 %collective-permute-done.7 = f32[28,128]{1,0:T(8,128)S(1)} collective-permute-done((f32[28,128]{1,0:T(8,128)S(1)}, f32[28,128]{1,0:T(8,128)S(1)}, u32[]{:S(2)}, u32[]{:S(2)}) %collective-permute-start.7) | collective-permute-done | bytes 14368 | tf_op jit(solution)/shard_map/ppermute | solution.py:277
  31.0 2.1 %collective-permute-start.8 = (f32[28,128]{1,0:T(8,128)S(1)}, f32[28,128]{1,0:T(8,128)S(1)}, u32[]{:S(2)}, u32[]{:S(2)}) collective-permute-start(f32[28,128]{1,0:T(8,128)S(1)} %add.22), channel_id=1, source_target_pairs={{0,8},{4,12},{8,0},{12,4},{16,24},{20,28},{24,16},{28,20},{1,9},{5... | collective-permute-start | bytes 43016 | tf_op jit(solution)/shard_map/ppermute | solution.py:277
  33.1 1.7 %collective-permute-done.8 = f32[28,128]{1,0:T(8,128)S(1)} collective-permute-done((f32[28,128]{1,0:T(8,128)S(1)}, f32[28,128]{1,0:T(8,128)S(1)}, u32[]{:S(2)}, u32[]{:S(2)}) %collective-permute-start.8) | collective-permute-done | bytes 14368 | tf_op jit(solution)/shard_map/ppermute | solution.py:277
  34.8 3.9 %collective-permute-start.9 = (f32[28,128]{1,0:T(8,128)S(1)}, f32[28,128]{1,0:T(8,128)S(1)}, u32[]{:S(2)}, u32[]{:S(2)}) collective-permute-start(f32[28,128]{1,0:T(8,128)S(1)} %add.23.merged_ref), channel_id=1, source_target_pairs={{0,16},{4,20},{8,24},{12,28},{16,0},{20,4},{24,8},{28,12},{1,17},{... | collective-permute-start | bytes 43016 | tf_op jit(solution)/shard_map/ppermute | solution.py:277
  38.7 1.7 %collective-permute-done.9.other_ref = f32[28,128]{1,0:T(8,128)S(1)} collective-permute-done((f32[28,128]{1,0:T(8,128)S(1)}, f32[28,128]{1,0:T(8,128)S(1)}, u32[]{:S(2)}, u32[]{:S(2)}) %collective-permute-start.9) | collective-permute-done | bytes 14368 | tf_op jit(solution)/shard_map/ppermute | solution.py:277
  40.4 1.0 %final.1 = (f32[3,512]{1,0:T(4,128)}, f32[3]{0:T(128)}) custom-call(f32[28,128]{1,0:T(8,128)S(1)} %add.23.merged_ref, f32[28,128]{1,0:T(8,128)S(1)} %collective-permute-done.9.other_ref), custom_call_target="tpu_custom_call" | custom-call | tf_op jit(solution)/shard_map/final/pallas_call | solution.py:347
  (5 shorter events, 0.1 us)
Async XLA Ops:
  4.7 9.4 %collective-permute-start.3 = (f32[32,16,128]{2,1,0:T(8,128)S(1)}, f32[32,16,128]{2,1,0:T(8,128)S(1)}, u32[]{:S(2)}, u32[]{:S(2)}) collective-permute-start(f32[32,16,128]{2,1,0:T(8,128)S(1)} %get-tuple-element.29), channel_id=1, source_target_pairs={{0,4},{4,0},{8,12},{12,8},{16,20},{20,16},{24,28},{28,24},{1,5},{5... | collective-permute-start | bytes 786440 | tf_op jit(solution)/shard_map/ppermute | solution.py:277
  11.1 8.5 %collective-permute-start.2 = (f32[32,16,128]{2,1,0:T(8,128)S(1)}, f32[32,16,128]{2,1,0:T(8,128)S(1)}, u32[]{:S(2)}, u32[]{:S(2)}) collective-permute-start(f32[32,16,128]{2,1,0:T(8,128)S(1)} %get-tuple-element.27), channel_id=1, source_target_pairs={{0,4},{4,0},{8,12},{12,8},{16,20},{20,16},{24,28},{28,24},{1,5},{5... | collective-permute-start | bytes 786440 | tf_op jit(solution)/shard_map/ppermute | solution.py:277
  14.2 14.1 %collective-permute-start.5 = (f32[16,16,128]{2,1,0:T(8,128)S(1)}, f32[16,16,128]{2,1,0:T(8,128)S(1)}, u32[]{:S(2)}, u32[]{:S(2)}) collective-permute-start(f32[16,16,128]{2,1,0:T(8,128)S(1)} %get-tuple-element.30), channel_id=1, source_target_pairs={{0,16},{4,20},{8,24},{12,28},{16,0},{20,4},{24,8},{28,12},{1,17},{... | collective-permute-start | bytes 393224 | tf_op jit(solution)/shard_map/ppermute | solution.py:331
  18.3 10.0 %collective-permute-start.4 = (f32[16,16,128]{2,1,0:T(8,128)S(1)}, f32[16,16,128]{2,1,0:T(8,128)S(1)}, u32[]{:S(2)}, u32[]{:S(2)}) collective-permute-start(f32[16,16,128]{2,1,0:T(8,128)S(1)} %get-tuple-element.31), channel_id=1, source_target_pairs={{0,24},{4,28},{8,16},{12,20},{16,8},{20,12},{24,0},{28,4},{1,25},{... | collective-permute-start | bytes 393224 | tf_op jit(solution)/shard_map/ppermute | solution.py:331
  19.7 9.4 %collective-permute-start.6 = (f32[16,16,128]{2,1,0:T(8,128)S(1)}, f32[16,16,128]{2,1,0:T(8,128)S(1)}, u32[]{:S(2)}, u32[]{:S(2)}) collective-permute-start(f32[16,16,128]{2,1,0:T(8,128)S(1)} %slice_add_fusion), channel_id=1, source_target_pairs={{0,8},{4,12},{8,0},{12,4},{16,24},{20,28},{24,16},{28,20},{1,9},{5... | collective-permute-start | bytes 393224 | tf_op jit(solution)/shard_map/ppermute | solution.py:331
  20.0 3.7 %collective-permute-start = (f32[16,128]{1,0:T(8,128)S(1)}, f32[16,128]{1,0:T(8,128)S(1)}, u32[]{:S(2)}, u32[]{:S(2)}) collective-permute-start(f32[16,128]{1,0:T(8,128)S(1)} %get-tuple-element.25), channel_id=1, source_target_pairs={{0,1},{1,0},{2,3},{3,2},{4,5},{5,4},{6,7},{7,6},{8,9},{9,8},{10,11... | collective-permute-start | bytes 24584 | tf_op jit(solution)/shard_map/ppermute | solution.py:277
  23.6 3.7 %collective-permute-start.1 = (f32[16,128]{1,0:T(8,128)S(1)}, f32[16,128]{1,0:T(8,128)S(1)}, u32[]{:S(2)}, u32[]{:S(2)}) collective-permute-start(f32[16,128]{1,0:T(8,128)S(1)} %add.18.tile_ref), channel_id=1, source_target_pairs={{0,2},{1,3},{2,0},{3,1},{4,6},{5,7},{6,4},{7,5},{8,10},{9,11},{10,... | collective-permute-start | bytes 24584 | tf_op jit(solution)/shard_map/ppermute | solution.py:277
  29.7 1.2 %collective-permute-start.7 = (f32[28,128]{1,0:T(8,128)S(1)}, f32[28,128]{1,0:T(8,128)S(1)}, u32[]{:S(2)}, u32[]{:S(2)}) collective-permute-start(f32[28,128]{1,0:T(8,128)S(1)} %levels.1), channel_id=1, source_target_pairs={{0,4},{4,0},{8,12},{12,8},{16,20},{20,16},{24,28},{28,24},{1,5},{5... | collective-permute-start | bytes 43016 | tf_op jit(solution)/shard_map/ppermute | solution.py:277
  31.0 3.8 %collective-permute-start.8 = (f32[28,128]{1,0:T(8,128)S(1)}, f32[28,128]{1,0:T(8,128)S(1)}, u32[]{:S(2)}, u32[]{:S(2)}) collective-permute-start(f32[28,128]{1,0:T(8,128)S(1)} %add.22), channel_id=1, source_target_pairs={{0,8},{4,12},{8,0},{12,4},{16,24},{20,28},{24,16},{28,20},{1,9},{5... | collective-permute-start | bytes 43016 | tf_op jit(solution)/shard_map/ppermute | solution.py:277
  34.8 5.7 %collective-permute-start.9 = (f32[28,128]{1,0:T(8,128)S(1)}, f32[28,128]{1,0:T(8,128)S(1)}, u32[]{:S(2)}, u32[]{:S(2)}) collective-permute-start(f32[28,128]{1,0:T(8,128)S(1)} %add.23.merged_ref), channel_id=1, source_target_pairs={{0,16},{4,20},{8,24},{12,28},{16,0},{20,4},{24,8},{28,12},{1,17},{... | collective-permute-start | bytes 43016 | tf_op jit(solution)/shard_map/ppermute | solution.py:277
